TPU v7x, 128 devices: a whole 4x4x4 slice. The times are simulated.
128 devices in a mesh: dp: 8 (over z_hi, y), tensor: 16 (over z_lo, x, core).
Axes of the slice: x: 4, y: 4, z: 4 (z_hi: 2, z_lo: 2; z = z_hi * 2 + z_lo), core: 2. Of those that a mesh axis runs over, the one named last changes fastest.
Arguments:
- normed_input: bfloat16 [8192, 8192], P('dp', 'tensor'), may hold values from -6 to 6
- positions: int32 [8192], P('dp'), may hold values from 0 to 8191
- fixed_weight_matrix: bfloat16 [8192, 10240], P('dp', 'tensor'), may hold values from -0.09375 to 0.09375
- adapter_down_map: bfloat16 [8192, 16], P('tensor'), may hold values from -0.0625 to 0.0625
- adapter_up_map: bfloat16 [16, 10240], P(None, 'tensor'), may hold values from -0.0625 to 0.0625
- output_gradient: bfloat16 [8192, 10240], P('dp', 'tensor'), may hold values from -6 to 6
Outputs:
- grad_x: bfloat16 [8192, 8192], P('dp', 'tensor')
- grad_a: float32 [8192, 16], P('tensor')
- grad_b: float32 [16, 10240], P(None, 'tensor')
All inputs are finite; a program needn't handle non-finite values.
Results may differ from a plain program's by a relative error of at most 0.0048.
Values may be sent and summed in bfloat16 or wider, within the bound.
No kernel may reach another device: no remote copies, remote signals or barrier semaphores. Data moves between devices by JAX's collectives and lax.ppermute only.
A program may use at most 256 MiB of HBM per device.

v0:
```python
import functools
import math

import jax
import jax.numpy as jnp
from jax import lax
from jax.experimental import pallas as pl
from jax.experimental.pallas import tpu as pltpu
from jax.sharding import PartitionSpec as P


HEAD = 128
K_SHARD = 64
RANK = 16
AXES = ("dp", "tensor")
BF16 = jnp.bfloat16
F32 = jnp.float32


def number(x, y, z, k):
    return ((z // 2) * 4 + y) * 16 + (z % 2) * 8 + x * 2 + k


CHIPS = [(x, y, z, k) for x in range(4) for y in range(4) for z in range(4) for k in range(2)]


def send(value, dx=0, dy=0, dk=0, zx=0, xx=0, yx=0, zmap=None):
    pairs = []
    for x, y, z, k in CHIPS:
        if zmap is None:
            to = z ^ zx
        elif z in zmap:
            to = zmap[z]
        else:
            continue
        pairs.append(
            (number(x, y, z, k), number(((x + dx) % 4) ^ xx, ((y + dy) % 4) ^ yx, to, k ^ dk))
        )
    return lax.ppermute(value, AXES, pairs)


def nt(a, b):
    return lax.dot_general(a, b, (((1,), (1,)), ((), ())), preferred_element_type=F32)


def place():
    dp, tensor = lax.axis_index("dp"), lax.axis_index("tensor")
    return dp // 4, dp % 4, tensor // 8, (tensor // 2) % 4, tensor % 2


def rotate_kernel(g_ref, cos_ref, sin_ref, swap_ref, x_ref, down_ref, up_ref, y_ref, low_ref):
    cosine = cos_ref[...]
    sine = sin_ref[...]
    odd = (lax.axis_index("tensor") * K_SHARD) % HEAD == K_SHARD
    lane = lax.broadcasted_iota(jnp.int32, cosine.shape, 1)
    key_cos = jnp.where(odd, pltpu.roll(cosine, 64, 1), cosine)
    key_sin = jnp.where(odd, pltpu.roll(sine, 64, 1), sine)
    key_cos = jnp.where(lane < K_SHARD, key_cos, 1.0)
    key_sin = jnp.where(lane < K_SHARD, key_sin, 0.0)
    groups = g_ref.shape[1] // HEAD
    for i in range(groups):
        g = g_ref[:, i * HEAD : (i + 1) * HEAD]
        turned = jnp.dot(g, swap_ref[...], preferred_element_type=F32)
        c = cosine if i < groups - 1 else key_cos
        s = sine if i < groups - 1 else key_sin
        y_ref[:, i * HEAD : (i + 1) * HEAD] = (g.astype(F32) * c + turned * s).astype(BF16)
    low_ref[:RANK, :] = nt(down_ref[...], x_ref[...])
    low_ref[RANK:, :] = nt(up_ref[...], y_ref[...])


def rotate(g, cosine, sine, swap, x, down_t, up):
    rows, width = g.shape
    block = 256
    spec = lambda cols: pl.BlockSpec((block, cols), lambda i: (i, 0))
    whole = lambda a: pl.BlockSpec(a.shape, lambda i: (0, 0))
    return pl.pallas_call(
        rotate_kernel,
        grid=(rows // block,),
        in_specs=[
            spec(width),
            spec(HEAD),
            spec(HEAD),
            whole(swap),
            spec(x.shape[1]),
            whole(down_t),
            whole(up),
        ],
        out_specs=[spec(width), pl.BlockSpec((2 * RANK, block), lambda i: (0, i))],
        out_shape=[
            jax.ShapeDtypeStruct((rows, width), BF16),
            jax.ShapeDtypeStruct((2 * RANK, rows), F32),
        ],
        compiler_params=pltpu.CompilerParams(
            dimension_semantics=("arbitrary",), vmem_limit_bytes=12 << 20
        ),
        cost_estimate=pl.CostEstimate(
            flops=2 * rows * width * 160, bytes_accessed=8 * rows * width, transcendentals=0
        ),
    )(g, cosine, sine, swap, x, down_t, up)


def product_kernel(chunks, adds, *refs):
    a_refs, b_refs, pieces = refs[:chunks], refs[chunks : 2 * chunks], refs[2 * chunks :]
    out_refs = refs[-2:] if adds else refs[-1:]
    _, y, _, x, k = place()
    core = k if adds else 1 - k
    block = 512
    rows = block * 2
    each = a_refs[0].shape[0] // block
    for i in range(rows // block):
        at = pl.ds((i % each) * block, block)
        left = jnp.concatenate([a_refs[i // each][at, :], b_refs[i // each][at, :]], axis=1)
        for r in range(4):
            if r == 2:
                from_prev, from_next = pieces[4], pieces[5]
                kept = jnp.concatenate([from_prev[0, core], from_next[0, core]], axis=0)
                other = jnp.concatenate([from_prev[1, core], from_next[1, core]], axis=0)
            else:
                first = {0: 0, 1: 2, 3: 6}[r]
                kept, other = pieces[first][core], pieces[first + 1][core]
            total = nt(left, jnp.concatenate([kept, other], axis=1))
            to = (y + r + 4 - x) % 4
            if adds:
                total = total + refs[-3][to, i * block : (i + 1) * block, :].astype(F32)
                out_refs[i][to] = total.astype(BF16)
            else:
                out_refs[0][to, i * block : (i + 1) * block, :] = total.astype(BF16)


def product(a, b, pieces, extra=None):
    rows = sum(c.shape[0] for c in a)
    width = a[0].shape[1]
    cols = pieces[0].shape[1]
    args = [*a, *b, *pieces]
    if extra is not None:
        args.append(extra)
    vmem = pl.BlockSpec(memory_space=pltpu.VMEM)
    return pl.pallas_call(
        functools.partial(product_kernel, len(a), extra is not None),
        in_specs=[vmem] * len(args),
        out_specs=vmem if extra is None else [vmem] * 2,
        out_shape=jax.ShapeDtypeStruct((4, rows, cols), BF16)
        if extra is None
        else [jax.ShapeDtypeStruct((4, rows // 2, cols), BF16)] * 2,
        compiler_params=pltpu.CompilerParams(vmem_limit_bytes=16 << 20),
        cost_estimate=pl.CostEstimate(
            flops=2 * rows * 2 * width * 4 * cols,
            bytes_accessed=2 * (2 * rows * width + 8 * cols * width + 4 * rows * cols),
            transcendentals=0,
        ),
    )(*args)


def adapters_kernel(factor, low_ref, more_ref, x_ref, y_ref, low_out, parts_ref):
    low = (low_ref[...] + more_ref[...]).astype(BF16)
    low_out[...] = low
    depth = x_ref.shape[1]
    parts_ref[:, :depth] = factor * jnp.dot(low[RANK:], x_ref[...], preferred_element_type=F32)
    parts_ref[:, depth:] = factor * jnp.dot(low[:RANK], y_ref[...], preferred_element_type=F32)


def adapters(factor, low, more, x, grad_y):
    vmem = pl.BlockSpec(memory_space=pltpu.VMEM)
    cols = x.shape[1] + grad_y.shape[1]
    return pl.pallas_call(
        functools.partial(adapters_kernel, factor),
        in_specs=[vmem] * 4,
        out_specs=[vmem] * 2,
        out_shape=[
            jax.ShapeDtypeStruct(low.shape, BF16),
            jax.ShapeDtypeStruct((RANK, cols), F32),
        ],
        compiler_params=pltpu.CompilerParams(vmem_limit_bytes=12 << 20),
        cost_estimate=pl.CostEstimate(
            flops=16 * RANK * x.shape[0] * cols, bytes_accessed=2 * x.shape[0] * cols, transcendentals=0
        ),
    )(low, more, x, grad_y)


def finish_kernel(own_ref, own_moved_ref, far_moved_ref, near_moved_ref, low_ref, down_ref, out_ref):
    zh, _, zl, _, _ = place()
    stays = zh == zl
    first = jnp.where(stays, own_ref[...], far_moved_ref[...])
    second = jnp.where(stays, own_moved_ref[...], near_moved_ref[...])
    adapter = 2.0 * lax.dot_general(
        low_ref[RANK:], down_ref[...], (((0,), (0,)), ((), ())), preferred_element_type=F32
    )
    cols = own_ref.shape[1]
    left = jnp.where(zl == 0, first, second)
    right = jnp.where(zl == 0, second, first)
    out_ref[:, :cols] = (left.astype(F32) + adapter[:, :cols]).astype(BF16)
    out_ref[:, cols:] = (right.astype(F32) + adapter[:, cols:]).astype(BF16)


def finish(own, own_moved, far_moved, near_moved, low, down_t):
    rows, cols = own.shape
    block = 256
    half = pl.BlockSpec((block, cols), lambda i: (i, 0))
    return pl.pallas_call(
        finish_kernel,
        grid=(rows // block,),
        in_specs=[half] * 4
        + [
            pl.BlockSpec((2 * RANK, block), lambda i: (0, i)),
            pl.BlockSpec(down_t.shape, lambda i: (0, 0)),
        ],
        out_specs=pl.BlockSpec((block, 2 * cols), lambda i: (i, 0)),
        out_shape=jax.ShapeDtypeStruct((rows, 2 * cols), BF16),
        compiler_params=pltpu.CompilerParams(
            dimension_semantics=("arbitrary",), vmem_limit_bytes=8 << 20
        ),
        cost_estimate=pl.CostEstimate(
            flops=64 * rows * cols, bytes_accessed=12 * rows * cols, transcendentals=0
        ),
    )(own, own_moved, far_moved, near_moved, low, down_t)


def reduce_over_x(top, low):
    far_up = send(top[2], dx=1)
    far_down = send(low[2], dx=-1)
    up_low = send(low[1], dx=1)
    down_top = send(top[3], dx=-1)
    up_top = send((top[1].astype(F32) + far_up.astype(F32)).astype(BF16), dx=1)
    down_low = send((low[3].astype(F32) + far_down.astype(F32)).astype(BF16), dx=-1)
    first = top[0].astype(F32) + up_top.astype(F32) + down_top.astype(F32)
    second = low[0].astype(F32) + up_low.astype(F32) + down_low.astype(F32)
    return jnp.concatenate([first, second], axis=0)


def in_order(normed_input, positions, weight, down, up, gradient):
    rows, width = gradient.shape
    zl = lax.axis_index("tensor") // 8

    quarters = weight.reshape(2, 2, weight.shape[0] // 4, width)
    kept = lax.dynamic_index_in_dim(quarters, zl, 1, keepdims=False)
    given = lax.dynamic_index_in_dim(quarters, 1 - zl, 1, keepdims=False)
    other = send(given, zx=1)
    half = kept.shape[1] // 2
    k_prev, k_next = send(kept, dy=1), send(kept, dy=-1)
    o_prev, o_next = send(other, dy=1), send(other, dy=-1)
    far_prev = send(jnp.stack([k_prev[:, :half], o_prev[:, :half]]), dy=1)
    far_next = send(jnp.stack([k_next[:, half:], o_next[:, half:]]), dy=-1)
    pieces = (kept, other, k_next, o_next, far_prev, far_next, k_prev, o_prev)

    lanes = jnp.arange(HEAD, dtype=jnp.int32)
    pair = (lanes // 2).astype(F32)
    freq = jnp.float32(500000.0) ** (-2.0 * pair / HEAD)
    angle = positions.astype(F32)[:, None] * freq[None, :]
    row, col = lanes[:, None], lanes[None, :]
    swap = jnp.where(row == (col ^ 1), jnp.where(col % 2 == 0, 1.0, -1.0), 0.0).astype(BF16)
    cosine, sine, down_t = jnp.cos(angle), jnp.sin(angle), down.T
    grad_y, low = rotate(gradient, cosine, sine, swap, normed_input, down_t, up)

    near = send(grad_y, zx=1)
    cross = send(grad_y, zx=3)
    mid = rows // 2
    far_top = send(cross[:mid], zx=1)
    far_low = send(near[mid:], zx=3)

    low = low + send(low, zx=1)
    low = low + send(low, dk=1)
    low = low + send(low, xx=1)
    more = send(low, xx=3)
    factor = 2.0 / math.sqrt(rows * 8)
    low, parts = adapters(factor, low, more, normed_input, grad_y)
    parts = parts + send(parts, yx=1)
    parts = parts + send(parts, yx=3)
    parts = parts + send(parts, zx=2)
    grad_a, grad_b = parts[:, : down.shape[0]].T, parts[:, down.shape[0] :]

    sums = []
    for a, b in (([grad_y], [near]), ([far_top, far_low], [cross])):
        if len(a) != len(b):
            b = [b[0][:mid], b[0][mid:]]
        partial = product(a, b, pieces)
        arrived = send(partial, dk=1)
        top, low_half = product(a, b, pieces, arrived)
        sums.append(reduce_over_x(top, low_half).astype(BF16))
    own, opposite = sums

    own_moved = send(own, zmap={1: 0, 2: 3})
    far_moved = send(opposite, zmap={0: 2, 3: 1})
    near_moved = send(opposite, zmap={1: 2, 2: 1})
    grad_x = finish(own, own_moved, far_moved, near_moved, low, down_t)
    return grad_x, grad_a, grad_b


def solution(mesh):
    placed = (
        P("dp", "tensor"),
        P("dp"),
        P("dp", "tensor"),
        P("tensor", None),
        P(None, "tensor"),
        P("dp", "tensor"),
    )
    return jax.shard_map(
        in_order,
        mesh=mesh,
        in_specs=placed,
        out_specs=(P("dp", "tensor"), P("tensor", None), P(None, "tensor")),
        check_vma=False,
    )
```

profile of v0, /device:TPU:32, one launch (start us, length us, event | category | flops | bytes accessed | tf_op | source)
XLA Modules:
  0.0 159.1 jit_solution(14203051725034355761)
XLA Ops:
  0.7 1.6 dynamic-slice_bitcast_fusion
  2.4 3.1 %collective-permute-start.2 = (bf16[2,256,640]{2,1,0:T(8,128)(2,1)S(1)}, bf16[2,256,640]{2,1,0:T(8,128)(2,1)S(1)}, u32[]{:S(2)}, u32[]{:S(2)}) collective-permute-start(bf16[2,256,640]{2,1,0:T(8,128)(2,1)S(1)} %get-tuple-element.22.refs_2_.refs_4_), channel_id=1, source_target_pairs={{0,48},{1,49},{8,56},{9,57},{64,112},{65,113},{72,120},{73,121},{1... | collective-permute-start | bytes 1966088 | tf_op jit(solution)/shard_map/ppermute | solution.py:39
  5.5 1.9 %multiply_sine_fusion = (f32[1024,128]{1,0:T(8,128)S(1)}, f32[1024,128]{1,0:T(8,128)S(1)}) fusion(f32[128]{0:T(128)S(1)} %fusion.14, f32[1024]{0:T(1024)S(1)} %convert_element_type.111), kind=kLoop, calls=%fused_computation | loop fusion | flops 131072 | bytes 1053184 | tf_op jit(solution)/shard_map/sin | solution.py:251
  7.4 11.4 %collective-permute-done.1.refs_3_.refs_5_ = bf16[2,256,640]{2,1,0:T(8,128)(2,1)S(1)} collective-permute-done((bf16[2,256,640]{2,1,0:T(8,128)(2,1)S(1)}, bf16[2,256,640]{2,1,0:T(8,128)(2,1)S(1)}, u32[]{:S(2)}, u32[]{:S(2)}) %collective-permute-start.1) | collective-permute-done | bytes 655392 | tf_op jit(solution)/shard_map/ppermute | solution.py:39
  18.8 1.6 collective-permute-start.5
  20.5 2.2 %shard_map.85 = (bf16[1024,640]{1,0:T(8,128)(2,1)S(1)}, f32[32,1024]{1,0:T(8,128)S(1)}) custom-call(bf16[1024,640]{1,0:T(8,128)(2,1)S(1)} %copy-done.1, f32[1024,128]{1,0:T(8,128)S(1)} %get-tuple-element.32.cos_ref, f32[1024,128]{1,0:T(8,128)S(1)} %get-tuple-element.31.sin_ref, bf16[128,128]{1,0:T(8,128)(2,1)S(1)} %select_convert_fusion.swap_ref, ...), custom_call_target="tpu_custom_call" | custom-call | flops 209715200 | bytes 5242880 | tf_op jit(solution)/shard_map/pallas_call | solution.py:76
  22.9 3.3 %collective-permute-start.16 = (bf16[1024,640]{1,0:T(8,128)(2,1)S(1)}, bf16[1024,640]{1,0:T(8,128)(2,1)S(1)}, u32[]{:S(2)}, u32[]{:S(2)}) collective-permute-start(bf16[1024,640]{1,0:T(8,128)(2,1)S(1)} %get-tuple-element.11.refs_0_.y_ref), channel_id=1, source_target_pairs={{0,72},{1,73},{8,64},{9,65},{64,8},{65,9},{72,0},{73,1},{16,88},{1... | collective-permute-start | bytes 3932168 | tf_op jit(solution)/shard_map/ppermute | solution.py:39
  26.2 1.7 %collective-permute-start.3 = (bf16[2,256,640]{2,1,0:T(8,128)(2,1)S(1)}, bf16[2,256,640]{2,1,0:T(8,128)(2,1)S(1)}, u32[]{:S(2)}, u32[]{:S(2)}) collective-permute-start(bf16[2,256,640]{2,1,0:T(8,128)(2,1)S(1)} %collective-permute-done.1.refs_3_.refs_5_), channel_id=1, source_target_pairs={{0,48},{1,49},{8,56},{9,57},{64,112},{65,113},{72,120},{73,121},{1... | collective-permute-start | bytes 1966088 | tf_op jit(solution)/shard_map/ppermute | solution.py:39
  27.9 9.0 %collective-permute-done.5.refs_9_.refs_11_ = bf16[2,256,640]{2,1,0:T(8,128)(2,1)S(1)} collective-permute-done((bf16[2,256,640]{2,1,0:T(8,128)(2,1)S(1)}, bf16[2,256,640]{2,1,0:T(8,128)(2,1)S(1)}, u32[]{:S(2)}, u32[]{:S(2)}) %collective-permute-start.5) | collective-permute-done | bytes 655392 | tf_op jit(solution)/shard_map/ppermute | solution.py:39
  37.1 3.9 %collective-permute-done.3.refs_5_.refs_7_ = bf16[2,256,640]{2,1,0:T(8,128)(2,1)S(1)} collective-permute-done((bf16[2,256,640]{2,1,0:T(8,128)(2,1)S(1)}, bf16[2,256,640]{2,1,0:T(8,128)(2,1)S(1)}, u32[]{:S(2)}, u32[]{:S(2)}) %collective-permute-start.3) | collective-permute-done | bytes 655392 | tf_op jit(solution)/shard_map/ppermute | solution.py:39
  41.1 3.0 %collective-permute-start.7 = (bf16[2,2,128,640]{3,2,1,0:T(8,128)(2,1)S(1)}, bf16[2,2,128,640]{3,2,1,0:T(8,128)(2,1)S(1)}, u32[]{:S(2)}, u32[]{:S(2)}) collective-permute-start(bf16[2,2,128,640]{3,2,1,0:T(8,128)(2,1)S(1)} %pad_maximum_fusion.1), channel_id=1, source_target_pairs={{0,48},{1,49},{8,56},{9,57},{64,112},{65,113},{72,120},{73,121},{1... | collective-permute-start | bytes 1966088 | tf_op jit(solution)/shard_map/ppermute | solution.py:39
  44.1 9.5 %collective-permute-done.16 = bf16[1024,640]{1,0:T(8,128)(2,1)S(1)} collective-permute-done((bf16[1024,640]{1,0:T(8,128)(2,1)S(1)}, bf16[1024,640]{1,0:T(8,128)(2,1)S(1)}, u32[]{:S(2)}, u32[]{:S(2)}) %collective-permute-start.16) | collective-permute-done | bytes 1310752 | tf_op jit(solution)/shard_map/ppermute | solution.py:39
  53.7 1.5 collective-permute-start.17
  55.2 2.0 %collective-permute-start.18 = (bf16[512,640]{1,0:T(8,128)(2,1)S(1)}, bf16[512,640]{1,0:T(8,128)(2,1)S(1)}, u32[]{:S(2)}, u32[]{:S(2)}) collective-permute-start(bf16[512,640]{1,0:T(8,128)(2,1)S(1)} %slice.106), channel_id=1, source_target_pairs={{0,72},{1,73},{8,64},{9,65},{64,8},{65,9},{72,0},{73,1},{16,88},{1... | collective-permute-start | bytes 1966088 | tf_op jit(solution)/shard_map/ppermute | solution.py:39
  57.2 3.0 %shard_map.86 = bf16[4,1024,256]{2,1,0:T(8,128)(2,1)S(1)} custom-call(bf16[1024,640]{1,0:T(8,128)(2,1)S(1)} %get-tuple-element.11.refs_0_.y_ref, bf16[1024,640]{1,0:T(8,128)(2,1)S(1)} %collective-permute-done.refs_1_, bf16[2,256,640]{2,1,0:T(8,128)(2,1)S(1)} %get-tuple-element.22.refs_2_.refs_4_, ...), custom_call_target="tpu_custom_call" | custom-call | flops 2684354560 | bytes 7340032 | tf_op jit(solution)/shard_map/pallas_call | solution.py:138
  60.4 7.9 %collective-permute-done.17.refs_0_ = bf16[512,640]{1,0:T(8,128)(2,1)S(1)} collective-permute-done((bf16[512,640]{1,0:T(8,128)(2,1)S(1)}, bf16[512,640]{1,0:T(8,128)(2,1)S(1)}, u32[]{:S(2)}, u32[]{:S(2)}) %collective-permute-start.17) | collective-permute-done | bytes 655392 | tf_op jit(solution)/shard_map/ppermute | solution.py:39
  69.4 3.0 %shard_map.88 = bf16[4,1024,256]{2,1,0:T(8,128)(2,1)S(1)} custom-call(bf16[512,640]{1,0:T(8,128)(2,1)S(1)} %collective-permute-done.17.refs_0_, bf16[512,640]{1,0:T(8,128)(2,1)S(1)} %collective-permute-done.18.refs_1_, bf16[512,640]{1,0:T(8,128)(2,1)S(1)} %get-tuple-element.20.refs_2_, bf16[512,640]{1,0:T(8,128)(2,1)S(1)} %get-tuple-element.19.refs_3_, ...), custom_call_target="tpu_custom_call" | custom-call | flops 2684354560 | bytes 7340032 | tf_op jit(solution)/shard_map/pallas_call | solution.py:138
  72.5 2.0 %collective-permute-start.28 = (f32[32,1024]{1,0:T(8,128)S(1)}, f32[32,1024]{1,0:T(8,128)S(1)}, u32[]{:S(2)}, u32[]{:S(2)}) collective-permute-start(f32[32,1024]{1,0:T(8,128)S(1)} %get-tuple-element.16), channel_id=1, source_target_pairs={{0,8},{1,9},{8,0},{9,1},{64,72},{65,73},{72,64},{73,65},{16,24},{1... | collective-permute-start | bytes 393224 | tf_op jit(solution)/shard_map/ppermute | solution.py:39
  74.5 4.1 %collective-permute-done.28 = f32[32,1024]{1,0:T(8,128)S(1)} collective-permute-done((f32[32,1024]{1,0:T(8,128)S(1)}, f32[32,1024]{1,0:T(8,128)S(1)}, u32[]{:S(2)}, u32[]{:S(2)}) %collective-permute-start.28) | collective-permute-done | bytes 131104 | tf_op jit(solution)/shard_map/ppermute | solution.py:39
  78.7 1.3 collective-permute-done.29
  80.0 1.6 collective-permute-start.30
  81.6 4.1 %collective-permute-done.30 = f32[32,1024]{1,0:T(8,128)S(1)} collective-permute-done((f32[32,1024]{1,0:T(8,128)S(1)}, f32[32,1024]{1,0:T(8,128)S(1)}, u32[]{:S(2)}, u32[]{:S(2)}) %collective-permute-start.30) | collective-permute-done | bytes 131104 | tf_op jit(solution)/shard_map/ppermute | solution.py:39
  85.7 3.0 %collective-permute-start.31 = (f32[32,1024]{1,0:T(8,128)S(1)}, f32[32,1024]{1,0:T(8,128)S(1)}, u32[]{:S(2)}, u32[]{:S(2)}) collective-permute-start(f32[32,1024]{1,0:T(8,128)S(1)} %add.96.low_ref), channel_id=1, source_target_pairs={{0,6},{1,7},{8,14},{9,15},{64,70},{65,71},{72,78},{73,79},{16,22},... | collective-permute-start | bytes 393224 | tf_op jit(solution)/shard_map/ppermute | solution.py:39
  88.7 3.0 %shard_map.87 = (bf16[4,512,256]{2,1,0:T(8,128)(2,1)S(1)}, bf16[4,512,256]{2,1,0:T(8,128)(2,1)S(1)}) custom-call(bf16[1024,640]{1,0:T(8,128)(2,1)S(1)} %get-tuple-element.11.refs_0_.y_ref, bf16[1024,640]{1,0:T(8,128)(2,1)S(1)} %collective-permute-done.refs_1_, bf16[2,256,640]{2,1,0:T(8,128)(2,1)S(1)} %get-tuple-element.22.refs_2_.refs_4_, ...), custom_call_target="tpu_custom_call" | custom-call | flops 2684354560 | bytes 7340032 | tf_op jit(solution)/shard_map/pallas_call | solution.py:138
  92.3 1.6 collective-permute-start.12
  93.9 1.7 %collective-permute-start.11 = (bf16[512,256]{1,0:T(8,128)(2,1)S(1)}, bf16[512,256]{1,0:T(8,128)(2,1)S(1)}, u32[]{:S(2)}, u32[]{:S(2)}) collective-permute-start(bf16[512,256]{1,0:T(8,128)(2,1)S(1)} %get-tuple-element.28), channel_id=1, source_target_pairs={{0,6},{1,7},{8,14},{9,15},{64,70},{65,71},{72,78},{73,79},{16,22},... | collective-permute-start | bytes 786440 | tf_op jit(solution)/shard_map/ppermute | solution.py:39
  96.0 3.0 %shard_map.89 = (bf16[4,512,256]{2,1,0:T(8,128)(2,1)S(1)}, bf16[4,512,256]{2,1,0:T(8,128)(2,1)S(1)}) custom-call(bf16[512,640]{1,0:T(8,128)(2,1)S(1)} %collective-permute-done.17.refs_0_, bf16[512,640]{1,0:T(8,128)(2,1)S(1)} %collective-permute-done.18.refs_1_, bf16[512,640]{1,0:T(8,128)(2,1)S(1)} %get-tuple-element.20.refs_2_, ...), custom_call_target="tpu_custom_call" | custom-call | flops 2684354560 | bytes 7340032 | tf_op jit(solution)/shard_map/pallas_call | solution.py:138
  99.1 1.9 %collective-permute-done.13 = bf16[512,256]{1,0:T(8,128)(2,1)S(1)} collective-permute-done((bf16[512,256]{1,0:T(8,128)(2,1)S(1)}, bf16[512,256]{1,0:T(8,128)(2,1)S(1)}, u32[]{:S(2)}, u32[]{:S(2)}) %collective-permute-start.13) | collective-permute-done | bytes 262176 | tf_op jit(solution)/shard_map/ppermute | solution.py:39
  101.0 1.7 %collective-permute-start.24 = (bf16[512,256]{1,0:T(8,128)(2,1)S(1)}, bf16[512,256]{1,0:T(8,128)(2,1)S(1)}, u32[]{:S(2)}, u32[]{:S(2)}) collective-permute-start(bf16[512,256]{1,0:T(8,128)(2,1)S(1)} %get-tuple-element.26), channel_id=1, source_target_pairs={{0,6},{1,7},{8,14},{9,15},{64,70},{65,71},{72,78},{73,79},{16,22},... | collective-permute-start | bytes 786440 | tf_op jit(solution)/shard_map/ppermute | solution.py:39
  102.8 3.3 %collective-permute-done.9 = bf16[512,256]{1,0:T(8,128)(2,1)S(1)} collective-permute-done((bf16[512,256]{1,0:T(8,128)(2,1)S(1)}, bf16[512,256]{1,0:T(8,128)(2,1)S(1)}, u32[]{:S(2)}, u32[]{:S(2)}) %collective-permute-start.9) | collective-permute-done | bytes 262176 | tf_op jit(solution)/shard_map/ppermute | solution.py:39
  106.5 3.8 %collective-permute-done.24 = bf16[512,256]{1,0:T(8,128)(2,1)S(1)} collective-permute-done((bf16[512,256]{1,0:T(8,128)(2,1)S(1)}, bf16[512,256]{1,0:T(8,128)(2,1)S(1)}, u32[]{:S(2)}, u32[]{:S(2)}) %collective-permute-start.24) | collective-permute-done | bytes 262176 | tf_op jit(solution)/shard_map/ppermute | solution.py:39
  110.3 1.7 %collective-permute-start.14 = (bf16[512,256]{1,0:T(8,128)(2,1)S(1)}, bf16[512,256]{1,0:T(8,128)(2,1)S(1)}, u32[]{:S(2)}, u32[]{:S(2)}) collective-permute-start(bf16[512,256]{1,0:T(8,128)(2,1)S(1)} %fusion.6), channel_id=1, source_target_pairs={{0,6},{1,7},{8,14},{9,15},{64,70},{65,71},{72,78},{73,79},{16,22},... | collective-permute-start | bytes 786440 | tf_op jit(solution)/shard_map/ppermute | solution.py:39
  112.1 1.6 %collective-permute-done.20 = bf16[512,256]{1,0:T(8,128)(2,1)S(1)} collective-permute-done((bf16[512,256]{1,0:T(8,128)(2,1)S(1)}, bf16[512,256]{1,0:T(8,128)(2,1)S(1)}, u32[]{:S(2)}, u32[]{:S(2)}) %collective-permute-start.20) | collective-permute-done | bytes 262176 | tf_op jit(solution)/shard_map/ppermute | solution.py:39
  113.8 3.1 %collective-permute-done.14 = bf16[512,256]{1,0:T(8,128)(2,1)S(1)} collective-permute-done((bf16[512,256]{1,0:T(8,128)(2,1)S(1)}, bf16[512,256]{1,0:T(8,128)(2,1)S(1)}, u32[]{:S(2)}, u32[]{:S(2)}) %collective-permute-start.14) | collective-permute-done | bytes 262176 | tf_op jit(solution)/shard_map/ppermute | solution.py:39
  116.9 2.7 %collective-permute-start.22 = (bf16[512,256]{1,0:T(8,128)(2,1)S(1)}, bf16[512,256]{1,0:T(8,128)(2,1)S(1)}, u32[]{:S(2)}, u32[]{:S(2)}) collective-permute-start(bf16[512,256]{1,0:T(8,128)(2,1)S(1)} %get-tuple-element.24), channel_id=1, source_target_pairs={{0,6},{1,7},{8,14},{9,15},{64,70},{65,71},{72,78},{73,79},{16,22},... | collective-permute-start | bytes 786440 | tf_op jit(solution)/shard_map/ppermute | solution.py:39
  119.8 4.3 %collective-permute-done.10 = bf16[512,256]{1,0:T(8,128)(2,1)S(1)} collective-permute-done((bf16[512,256]{1,0:T(8,128)(2,1)S(1)}, bf16[512,256]{1,0:T(8,128)(2,1)S(1)}, u32[]{:S(2)}, u32[]{:S(2)}) %collective-permute-start.10) | collective-permute-done | bytes 262176 | tf_op jit(solution)/shard_map/ppermute | solution.py:39
  124.2 4.0 %collective-permute-done.23 = bf16[512,256]{1,0:T(8,128)(2,1)S(1)} collective-permute-done((bf16[512,256]{1,0:T(8,128)(2,1)S(1)}, bf16[512,256]{1,0:T(8,128)(2,1)S(1)}, u32[]{:S(2)}, u32[]{:S(2)}) %collective-permute-start.23) | collective-permute-done | bytes 262176 | tf_op jit(solution)/shard_map/ppermute | solution.py:39
  128.3 3.6 %collective-permute-start.15 = (bf16[1024,256]{1,0:T(8,128)(2,1)S(1)}, bf16[1024,256]{1,0:T(8,128)(2,1)S(1)}, u32[]{:S(2)}, u32[]{:S(2)}) collective-permute-start(bf16[1024,256]{1,0:T(8,128)(2,1)S(1)} %pad_maximum_fusion.2.own_ref), channel_id=1, source_target_pairs={{8,0},{9,1},{64,72},{65,73},{24,16},{25,17},{80,88},{81,89},{40,32... | collective-permute-start | bytes 1572872 | tf_op jit(solution)/shard_map/ppermute | solution.py:39
  132.2 1.3 collective-permute-start.26
  133.5 3.4 %collective-permute-start.27 = (bf16[1024,256]{1,0:T(8,128)(2,1)S(1)}, bf16[1024,256]{1,0:T(8,128)(2,1)S(1)}, u32[]{:S(2)}, u32[]{:S(2)}) collective-permute-start(bf16[1024,256]{1,0:T(8,128)(2,1)S(1)} %pad_maximum_fusion.3), channel_id=1, source_target_pairs={{8,64},{9,65},{64,8},{65,9},{24,80},{25,81},{80,24},{81,25},{40,96... | collective-permute-start | bytes 1572872 | tf_op jit(solution)/shard_map/ppermute | solution.py:39
  137.3 1.7 %collective-permute-start.32 = (f32[16,1152]{1,0:T(8,128)S(1)}, f32[16,1152]{1,0:T(8,128)S(1)}, u32[]{:S(2)}, u32[]{:S(2)}) collective-permute-start(f32[16,1152]{1,0:T(8,128)S(1)} %get-tuple-element.18), channel_id=1, source_target_pairs={{0,16},{1,17},{8,24},{9,25},{64,80},{65,81},{72,88},{73,89},{16,0}... | collective-permute-start | bytes 221192 | tf_op jit(solution)/shard_map/ppermute | solution.py:39
  139.0 2.7 %collective-permute-done.32 = f32[16,1152]{1,0:T(8,128)S(1)} collective-permute-done((f32[16,1152]{1,0:T(8,128)S(1)}, f32[16,1152]{1,0:T(8,128)S(1)}, u32[]{:S(2)}, u32[]{:S(2)}) %collective-permute-start.32) | collective-permute-done | bytes 73760 | tf_op jit(solution)/shard_map/ppermute | solution.py:39
  141.7 1.9 %collective-permute-start.33 = (f32[16,1152]{1,0:T(8,128)S(1)}, f32[16,1152]{1,0:T(8,128)S(1)}, u32[]{:S(2)}, u32[]{:S(2)}) collective-permute-start(f32[16,1152]{1,0:T(8,128)S(1)} %add.97), channel_id=1, source_target_pairs={{0,48},{1,49},{8,56},{9,57},{64,112},{65,113},{72,120},{73,121},{1... | collective-permute-start | bytes 221192 | tf_op jit(solution)/shard_map/ppermute | solution.py:39
  143.6 3.8 %collective-permute-done.33 = f32[16,1152]{1,0:T(8,128)S(1)} collective-permute-done((f32[16,1152]{1,0:T(8,128)S(1)}, f32[16,1152]{1,0:T(8,128)S(1)}, u32[]{:S(2)}, u32[]{:S(2)}) %collective-permute-start.33) | collective-permute-done | bytes 73760 | tf_op jit(solution)/shard_map/ppermute | solution.py:39
  147.4 1.6 collective-permute-start.34
  149.0 4.5 %collective-permute-done.34 = f32[16,1152]{1,0:T(8,128)S(1)} collective-permute-done((f32[16,1152]{1,0:T(8,128)S(1)}, f32[16,1152]{1,0:T(8,128)S(1)}, u32[]{:S(2)}, u32[]{:S(2)}) %collective-permute-start.34) | collective-permute-done | bytes 73760 | tf_op jit(solution)/shard_map/ppermute | solution.py:39
  154.7 2.2 %collective-permute-done.27.near_moved_ref = bf16[1024,256]{1,0:T(8,128)(2,1)S(1)} collective-permute-done((bf16[1024,256]{1,0:T(8,128)(2,1)S(1)}, bf16[1024,256]{1,0:T(8,128)(2,1)S(1)}, u32[]{:S(2)}, u32[]{:S(2)}) %collective-permute-start.27) | collective-permute-done | bytes 524320 | tf_op jit(solution)/shard_map/ppermute | solution.py:39
  156.9 2.2 %shard_map.91 = bf16[1024,512]{1,0:T(8,128)(2,1)} custom-call(bf16[1024,256]{1,0:T(8,128)(2,1)S(1)} %pad_maximum_fusion.2.own_ref, bf16[1024,256]{1,0:T(8,128)(2,1)S(1)} %collective-permute-done.15.own_moved_ref, bf16[1024,256]{1,0:T(8,128)(2,1)S(1)} %collective-permute-done.26.far_moved_ref, bf16[1024,256]{1,0:T(8,128)(2,1)S(1)} %collective-permute-done.27.near_moved_ref, ...), custom_call_target="tpu_custom_call" | custom-call | flops 16777216 | bytes 3145728 | tf_op jit(solution)/shard_map/pallas_call | solution.py:199
  (76 shorter events, 6.4 us)
Async XLA Ops:
  0.7 4.8 %copy-start.4 = (s32[1024]{0:T(1024)S(1)}, s32[1024]{0:T(1024)}, u32[]{:S(2)}) copy-start(s32[1024]{0:T(1024)} %param.7) | copy-start | bytes 12292
  0.7 19.7 %copy-start = (bf16[1024,512]{1,0:T(8,128)(2,1)S(1)}, bf16[1024,512]{1,0:T(8,128)(2,1)}, u32[]{:S(2)}) copy-start(bf16[1024,512]{1,0:T(8,128)(2,1)} %x_ref.3) | copy-start | bytes 3145732
  0.7 19.7 %copy-start.1 = (bf16[1024,640]{1,0:T(8,128)(2,1)S(1)}, bf16[1024,640]{1,0:T(8,128)(2,1)}, u32[]{:S(2)}) copy-start(bf16[1024,640]{1,0:T(8,128)(2,1)} %g_ref.1) | copy-start | bytes 3932164
  0.7 19.7 %copy-start.2 = (bf16[512,16]{0,1:T(8,128)(2,1)S(1)}, bf16[512,16]{0,1:T(8,128)(2,1)}, u32[]{:S(2)}) copy-start(bf16[512,16]{0,1:T(8,128)(2,1)} %param.9) | copy-start | bytes 49156
  0.7 19.7 %copy-start.3 = (bf16[16,640]{1,0:T(8,128)(2,1)S(1)}, bf16[16,640]{1,0:T(8,128)(2,1)}, u32[]{:S(2)}) copy-start(bf16[16,640]{1,0:T(8,128)(2,1)} %up_ref.1) | copy-start | bytes 61444
  2.3 16.6 %collective-permute-start.1 = (bf16[2,256,640]{2,1,0:T(8,128)(2,1)S(1)}, bf16[2,256,640]{2,1,0:T(8,128)(2,1)S(1)}, u32[]{:S(2)}, u32[]{:S(2)}) collective-permute-start(bf16[2,256,640]{2,1,0:T(8,128)(2,1)S(1)} %get-tuple-element.21), channel_id=1, source_target_pairs={{0,8},{1,9},{8,0},{9,1},{64,72},{65,73},{72,64},{73,65},{16,24},{1... | collective-permute-start | bytes 1966088 | tf_op jit(solution)/shard_map/ppermute | solution.py:39
  2.4 25.5 %collective-permute-start.2 = (bf16[2,256,640]{2,1,0:T(8,128)(2,1)S(1)}, bf16[2,256,640]{2,1,0:T(8,128)(2,1)S(1)}, u32[]{:S(2)}, u32[]{:S(2)}) collective-permute-start(bf16[2,256,640]{2,1,0:T(8,128)(2,1)S(1)} %get-tuple-element.22.refs_2_.refs_4_), channel_id=1, source_target_pairs={{0,48},{1,49},{8,56},{9,57},{64,112},{65,113},{72,120},{73,121},{1... | collective-permute-start | bytes 1966088 | tf_op jit(solution)/shard_map/ppermute | solution.py:39
  5.5 20.7 %collective-permute-start.4 = (bf16[2,256,640]{2,1,0:T(8,128)(2,1)S(1)}, bf16[2,256,640]{2,1,0:T(8,128)(2,1)S(1)}, u32[]{:S(2)}, u32[]{:S(2)}) collective-permute-start(bf16[2,256,640]{2,1,0:T(8,128)(2,1)S(1)} %get-tuple-element.22.refs_2_.refs_4_), channel_id=1, source_target_pairs={{0,16},{1,17},{8,24},{9,25},{64,80},{65,81},{72,88},{73,89},{16,32... | collective-permute-start | bytes 1966088 | tf_op jit(solution)/shard_map/ppermute | solution.py:39
  18.8 18.1 %collective-permute-start.5 = (bf16[2,256,640]{2,1,0:T(8,128)(2,1)S(1)}, bf16[2,256,640]{2,1,0:T(8,128)(2,1)S(1)}, u32[]{:S(2)}, u32[]{:S(2)}) collective-permute-start(bf16[2,256,640]{2,1,0:T(8,128)(2,1)S(1)} %collective-permute-done.1.refs_3_.refs_5_), channel_id=1, source_target_pairs={{0,16},{1,17},{8,24},{9,25},{64,80},{65,81},{72,88},{73,89},{16,32... | collective-permute-start | bytes 1966088 | tf_op jit(solution)/shard_map/ppermute | solution.py:39
  22.6 32.6 %collective-permute-start = (bf16[1024,640]{1,0:T(8,128)(2,1)S(1)}, bf16[1024,640]{1,0:T(8,128)(2,1)S(1)}, u32[]{:S(2)}, u32[]{:S(2)}) collective-permute-start(bf16[1024,640]{1,0:T(8,128)(2,1)S(1)} %get-tuple-element.11.refs_0_.y_ref), channel_id=1, source_target_pairs={{0,8},{1,9},{8,0},{9,1},{64,72},{65,73},{72,64},{73,65},{16,24},{1... | collective-permute-start | bytes 3932168 | tf_op jit(solution)/shard_map/ppermute | solution.py:39
  22.9 30.6 %collective-permute-start.16 = (bf16[1024,640]{1,0:T(8,128)(2,1)S(1)}, bf16[1024,640]{1,0:T(8,128)(2,1)S(1)}, u32[]{:S(2)}, u32[]{:S(2)}) collective-permute-start(bf16[1024,640]{1,0:T(8,128)(2,1)S(1)} %get-tuple-element.11.refs_0_.y_ref), channel_id=1, source_target_pairs={{0,72},{1,73},{8,64},{9,65},{64,8},{65,9},{72,0},{73,1},{16,88},{1... | collective-permute-start | bytes 3932168 | tf_op jit(solution)/shard_map/ppermute | solution.py:39
  26.2 14.8 %collective-permute-start.3 = (bf16[2,256,640]{2,1,0:T(8,128)(2,1)S(1)}, bf16[2,256,640]{2,1,0:T(8,128)(2,1)S(1)}, u32[]{:S(2)}, u32[]{:S(2)}) collective-permute-start(bf16[2,256,640]{2,1,0:T(8,128)(2,1)S(1)} %collective-permute-done.1.refs_3_.refs_5_), channel_id=1, source_target_pairs={{0,48},{1,49},{8,56},{9,57},{64,112},{65,113},{72,120},{73,121},{1... | collective-permute-start | bytes 1966088 | tf_op jit(solution)/shard_map/ppermute | solution.py:39
  37.0 20.2 %collective-permute-start.6 = (bf16[2,2,128,640]{3,2,1,0:T(8,128)(2,1)S(1)}, bf16[2,2,128,640]{3,2,1,0:T(8,128)(2,1)S(1)}, u32[]{:S(2)}, u32[]{:S(2)}) collective-permute-start(bf16[2,2,128,640]{3,2,1,0:T(8,128)(2,1)S(1)} %pad_maximum_fusion), channel_id=1, source_target_pairs={{0,16},{1,17},{8,24},{9,25},{64,80},{65,81},{72,88},{73,89},{16,32... | collective-permute-start | bytes 1966088 | tf_op jit(solution)/shard_map/ppermute | solution.py:39
  41.1 16.2 %collective-permute-start.7 = (bf16[2,2,128,640]{3,2,1,0:T(8,128)(2,1)S(1)}, bf16[2,2,128,640]{3,2,1,0:T(8,128)(2,1)S(1)}, u32[]{:S(2)}, u32[]{:S(2)}) collective-permute-start(bf16[2,2,128,640]{3,2,1,0:T(8,128)(2,1)S(1)} %pad_maximum_fusion.1), channel_id=1, source_target_pairs={{0,48},{1,49},{8,56},{9,57},{64,112},{65,113},{72,120},{73,121},{1... | collective-permute-start | bytes 1966088 | tf_op jit(solution)/shard_map/ppermute | solution.py:39
  53.7 14.6 %collective-permute-start.17 = (bf16[512,640]{1,0:T(8,128)(2,1)S(1)}, bf16[512,640]{1,0:T(8,128)(2,1)S(1)}, u32[]{:S(2)}, u32[]{:S(2)}) collective-permute-start(bf16[512,640]{1,0:T(8,128)(2,1)S(1)} %get-tuple-element.20.refs_2_), channel_id=1, source_target_pairs={{0,8},{1,9},{8,0},{9,1},{64,72},{65,73},{72,64},{73,65},{16,24},{1... | collective-permute-start | bytes 1966088 | tf_op jit(solution)/shard_map/ppermute | solution.py:39
  55.2 14.2 %collective-permute-start.18 = (bf16[512,640]{1,0:T(8,128)(2,1)S(1)}, bf16[512,640]{1,0:T(8,128)(2,1)S(1)}, u32[]{:S(2)}, u32[]{:S(2)}) collective-permute-start(bf16[512,640]{1,0:T(8,128)(2,1)S(1)} %slice.106), channel_id=1, source_target_pairs={{0,72},{1,73},{8,64},{9,65},{64,8},{65,9},{72,0},{73,1},{16,88},{1... | collective-permute-start | bytes 1966088 | tf_op jit(solution)/shard_map/ppermute | solution.py:39
  60.3 28.4 %collective-permute-start.8 = (bf16[4,1024,256]{2,1,0:T(8,128)(2,1)S(1)}, bf16[4,1024,256]{2,1,0:T(8,128)(2,1)S(1)}, u32[]{:S(2)}, u32[]{:S(2)}) collective-permute-start(bf16[4,1024,256]{2,1,0:T(8,128)(2,1)S(1)} %shard_map.86), channel_id=1, source_target_pairs={{0,1},{1,0},{8,9},{9,8},{64,65},{65,64},{72,73},{73,72},{16,17},{1... | collective-permute-start | bytes 6291464 | tf_op jit(solution)/shard_map/ppermute | solution.py:39
  72.4 23.2 %collective-permute-start.19 = (bf16[4,1024,256]{2,1,0:T(8,128)(2,1)S(1)}, bf16[4,1024,256]{2,1,0:T(8,128)(2,1)S(1)}, u32[]{:S(2)}, u32[]{:S(2)}) collective-permute-start(bf16[4,1024,256]{2,1,0:T(8,128)(2,1)S(1)} %shard_map.88), channel_id=1, source_target_pairs={{0,1},{1,0},{8,9},{9,8},{64,65},{65,64},{72,73},{73,72},{16,17},{1... | collective-permute-start | bytes 6291464 | tf_op jit(solution)/shard_map/ppermute | solution.py:39
  72.5 6.0 %collective-permute-start.28 = (f32[32,1024]{1,0:T(8,128)S(1)}, f32[32,1024]{1,0:T(8,128)S(1)}, u32[]{:S(2)}, u32[]{:S(2)}) collective-permute-start(f32[32,1024]{1,0:T(8,128)S(1)} %get-tuple-element.16), channel_id=1, source_target_pairs={{0,8},{1,9},{8,0},{9,1},{64,72},{65,73},{72,64},{73,65},{16,24},{1... | collective-permute-start | bytes 393224 | tf_op jit(solution)/shard_map/ppermute | solution.py:39
  78.6 1.4 collective-permute-start.29
  80.0 5.6 %collective-permute-start.30 = (f32[32,1024]{1,0:T(8,128)S(1)}, f32[32,1024]{1,0:T(8,128)S(1)}, u32[]{:S(2)}, u32[]{:S(2)}) collective-permute-start(f32[32,1024]{1,0:T(8,128)S(1)} %add.95), channel_id=1, source_target_pairs={{0,2},{1,3},{8,10},{9,11},{64,66},{65,67},{72,74},{73,75},{16,18},... | collective-permute-start | bytes 393224 | tf_op jit(solution)/shard_map/ppermute | solution.py:39
  85.7 51.2 %collective-permute-start.31 = (f32[32,1024]{1,0:T(8,128)S(1)}, f32[32,1024]{1,0:T(8,128)S(1)}, u32[]{:S(2)}, u32[]{:S(2)}) collective-permute-start(f32[32,1024]{1,0:T(8,128)S(1)} %add.96.low_ref), channel_id=1, source_target_pairs={{0,6},{1,7},{8,14},{9,15},{64,70},{65,71},{72,78},{73,79},{16,22},... | collective-permute-start | bytes 393224 | tf_op jit(solution)/shard_map/ppermute | solution.py:39
  91.8 9.2 %collective-permute-start.13 = (bf16[512,256]{1,0:T(8,128)(2,1)S(1)}, bf16[512,256]{1,0:T(8,128)(2,1)S(1)}, u32[]{:S(2)}, u32[]{:S(2)}) collective-permute-start(bf16[512,256]{1,0:T(8,128)(2,1)S(1)} %get-tuple-element.30), channel_id=1, source_target_pairs={{0,6},{1,7},{8,14},{9,15},{64,70},{65,71},{72,78},{73,79},{16,22},... | collective-permute-start | bytes 786440 | tf_op jit(solution)/shard_map/ppermute | solution.py:39
  92.3 21.4 %collective-permute-start.12 = (bf16[512,256]{1,0:T(8,128)(2,1)S(1)}, bf16[512,256]{1,0:T(8,128)(2,1)S(1)}, u32[]{:S(2)}, u32[]{:S(2)}) collective-permute-start(bf16[512,256]{1,0:T(8,128)(2,1)S(1)} %get-tuple-element.29), channel_id=1, source_target_pairs={{0,2},{1,3},{8,10},{9,11},{64,66},{65,67},{72,74},{73,75},{16,18},... | collective-permute-start | bytes 786440 | tf_op jit(solution)/shard_map/ppermute | solution.py:39
  93.9 25.8 %collective-permute-start.11 = (bf16[512,256]{1,0:T(8,128)(2,1)S(1)}, bf16[512,256]{1,0:T(8,128)(2,1)S(1)}, u32[]{:S(2)}, u32[]{:S(2)}) collective-permute-start(bf16[512,256]{1,0:T(8,128)(2,1)S(1)} %get-tuple-element.28), channel_id=1, source_target_pairs={{0,6},{1,7},{8,14},{9,15},{64,70},{65,71},{72,78},{73,79},{16,22},... | collective-permute-start | bytes 786440 | tf_op jit(solution)/shard_map/ppermute | solution.py:39
  95.6 10.4 %collective-permute-start.9 = (bf16[512,256]{1,0:T(8,128)(2,1)S(1)}, bf16[512,256]{1,0:T(8,128)(2,1)S(1)}, u32[]{:S(2)}, u32[]{:S(2)}) collective-permute-start(bf16[512,256]{1,0:T(8,128)(2,1)S(1)} %get-tuple-element.27), channel_id=1, source_target_pairs={{0,2},{1,3},{8,10},{9,11},{64,66},{65,67},{72,74},{73,75},{16,18},... | collective-permute-start | bytes 786440 | tf_op jit(solution)/shard_map/ppermute | solution.py:39
  101.0 9.3 %collective-permute-start.24 = (bf16[512,256]{1,0:T(8,128)(2,1)S(1)}, bf16[512,256]{1,0:T(8,128)(2,1)S(1)}, u32[]{:S(2)}, u32[]{:S(2)}) collective-permute-start(bf16[512,256]{1,0:T(8,128)(2,1)S(1)} %get-tuple-element.26), channel_id=1, source_target_pairs={{0,6},{1,7},{8,14},{9,15},{64,70},{65,71},{72,78},{73,79},{16,22},... | collective-permute-start | bytes 786440 | tf_op jit(solution)/shard_map/ppermute | solution.py:39
  106.1 7.6 %collective-permute-start.20 = (bf16[512,256]{1,0:T(8,128)(2,1)S(1)}, bf16[512,256]{1,0:T(8,128)(2,1)S(1)}, u32[]{:S(2)}, u32[]{:S(2)}) collective-permute-start(bf16[512,256]{1,0:T(8,128)(2,1)S(1)} %get-tuple-element.23), channel_id=1, source_target_pairs={{0,2},{1,3},{8,10},{9,11},{64,66},{65,67},{72,74},{73,75},{16,18},... | collective-permute-start | bytes 786440 | tf_op jit(solution)/shard_map/ppermute | solution.py:39
  110.3 6.6 %collective-permute-start.14 = (bf16[512,256]{1,0:T(8,128)(2,1)S(1)}, bf16[512,256]{1,0:T(8,128)(2,1)S(1)}, u32[]{:S(2)}, u32[]{:S(2)}) collective-permute-start(bf16[512,256]{1,0:T(8,128)(2,1)S(1)} %fusion.6), channel_id=1, source_target_pairs={{0,6},{1,7},{8,14},{9,15},{64,70},{65,71},{72,78},{73,79},{16,22},... | collective-permute-start | bytes 786440 | tf_op jit(solution)/shard_map/ppermute | solution.py:39
  113.7 10.4 %collective-permute-start.10 = (bf16[512,256]{1,0:T(8,128)(2,1)S(1)}, bf16[512,256]{1,0:T(8,128)(2,1)S(1)}, u32[]{:S(2)}, u32[]{:S(2)}) collective-permute-start(bf16[512,256]{1,0:T(8,128)(2,1)S(1)} %fusion.9), channel_id=1, source_target_pairs={{0,2},{1,3},{8,10},{9,11},{64,66},{65,67},{72,74},{73,75},{16,18},... | collective-permute-start | bytes 786440 | tf_op jit(solution)/shard_map/ppermute | solution.py:39
  113.8 14.5 %collective-permute-start.23 = (bf16[512,256]{1,0:T(8,128)(2,1)S(1)}, bf16[512,256]{1,0:T(8,128)(2,1)S(1)}, u32[]{:S(2)}, u32[]{:S(2)}) collective-permute-start(bf16[512,256]{1,0:T(8,128)(2,1)S(1)} %get-tuple-element.25), channel_id=1, source_target_pairs={{0,2},{1,3},{8,10},{9,11},{64,66},{65,67},{72,74},{73,75},{16,18},... | collective-permute-start | bytes 786440 | tf_op jit(solution)/shard_map/ppermute | solution.py:39
  116.9 15.1 %collective-permute-start.22 = (bf16[512,256]{1,0:T(8,128)(2,1)S(1)}, bf16[512,256]{1,0:T(8,128)(2,1)S(1)}, u32[]{:S(2)}, u32[]{:S(2)}) collective-permute-start(bf16[512,256]{1,0:T(8,128)(2,1)S(1)} %get-tuple-element.24), channel_id=1, source_target_pairs={{0,6},{1,7},{8,14},{9,15},{64,70},{65,71},{72,78},{73,79},{16,22},... | collective-permute-start | bytes 786440 | tf_op jit(solution)/shard_map/ppermute | solution.py:39
  119.7 12.2 %collective-permute-start.25 = (bf16[512,256]{1,0:T(8,128)(2,1)S(1)}, bf16[512,256]{1,0:T(8,128)(2,1)S(1)}, u32[]{:S(2)}, u32[]{:S(2)}) collective-permute-start(bf16[512,256]{1,0:T(8,128)(2,1)S(1)} %fusion), channel_id=1, source_target_pairs={{0,6},{1,7},{8,14},{9,15},{64,70},{65,71},{72,78},{73,79},{16,22},... | collective-permute-start | bytes 786440 | tf_op jit(solution)/shard_map/ppermute | solution.py:39
  124.1 8.0 %collective-permute-start.21 = (bf16[512,256]{1,0:T(8,128)(2,1)S(1)}, bf16[512,256]{1,0:T(8,128)(2,1)S(1)}, u32[]{:S(2)}, u32[]{:S(2)}) collective-permute-start(bf16[512,256]{1,0:T(8,128)(2,1)S(1)} %fusion.3), channel_id=1, source_target_pairs={{0,2},{1,3},{8,10},{9,11},{64,66},{65,67},{72,74},{73,75},{16,18},... | collective-permute-start | bytes 786440 | tf_op jit(solution)/shard_map/ppermute | solution.py:39
  128.3 26.4 %collective-permute-start.15 = (bf16[1024,256]{1,0:T(8,128)(2,1)S(1)}, bf16[1024,256]{1,0:T(8,128)(2,1)S(1)}, u32[]{:S(2)}, u32[]{:S(2)}) collective-permute-start(bf16[1024,256]{1,0:T(8,128)(2,1)S(1)} %pad_maximum_fusion.2.own_ref), channel_id=1, source_target_pairs={{8,0},{9,1},{64,72},{65,73},{24,16},{25,17},{80,88},{81,89},{40,32... | collective-permute-start | bytes 1572872 | tf_op jit(solution)/shard_map/ppermute | solution.py:39
  132.2 22.5 %collective-permute-start.26 = (bf16[1024,256]{1,0:T(8,128)(2,1)S(1)}, bf16[1024,256]{1,0:T(8,128)(2,1)S(1)}, u32[]{:S(2)}, u32[]{:S(2)}) collective-permute-start(bf16[1024,256]{1,0:T(8,128)(2,1)S(1)} %pad_maximum_fusion.3), channel_id=1, source_target_pairs={{0,64},{1,65},{72,8},{73,9},{16,80},{17,81},{88,24},{89,25},{32,96... | collective-permute-start | bytes 1572872 | tf_op jit(solution)/shard_map/ppermute | solution.py:39
  133.5 23.4 %collective-permute-start.27 = (bf16[1024,256]{1,0:T(8,128)(2,1)S(1)}, bf16[1024,256]{1,0:T(8,128)(2,1)S(1)}, u32[]{:S(2)}, u32[]{:S(2)}) collective-permute-start(bf16[1024,256]{1,0:T(8,128)(2,1)S(1)} %pad_maximum_fusion.3), channel_id=1, source_target_pairs={{8,64},{9,65},{64,8},{65,9},{24,80},{25,81},{80,24},{81,25},{40,96... | collective-permute-start | bytes 1572872 | tf_op jit(solution)/shard_map/ppermute | solution.py:39
  137.3 4.4 %collective-permute-start.32 = (f32[16,1152]{1,0:T(8,128)S(1)}, f32[16,1152]{1,0:T(8,128)S(1)}, u32[]{:S(2)}, u32[]{:S(2)}) collective-permute-start(f32[16,1152]{1,0:T(8,128)S(1)} %get-tuple-element.18), channel_id=1, source_target_pairs={{0,16},{1,17},{8,24},{9,25},{64,80},{65,81},{72,88},{73,89},{16,0}... | collective-permute-start | bytes 221192 | tf_op jit(solution)/shard_map/ppermute | solution.py:39
  141.7 5.6 %collective-permute-start.33 = (f32[16,1152]{1,0:T(8,128)S(1)}, f32[16,1152]{1,0:T(8,128)S(1)}, u32[]{:S(2)}, u32[]{:S(2)}) collective-permute-start(f32[16,1152]{1,0:T(8,128)S(1)} %add.97), channel_id=1, source_target_pairs={{0,48},{1,49},{8,56},{9,57},{64,112},{65,113},{72,120},{73,121},{1... | collective-permute-start | bytes 221192 | tf_op jit(solution)/shard_map/ppermute | solution.py:39
  147.4 6.0 %collective-permute-start.34 = (f32[16,1152]{1,0:T(8,128)S(1)}, f32[16,1152]{1,0:T(8,128)S(1)}, u32[]{:S(2)}, u32[]{:S(2)}) collective-permute-start(f32[16,1152]{1,0:T(8,128)S(1)} %add.98), channel_id=1, source_target_pairs={{0,64},{1,65},{8,72},{9,73},{64,0},{65,1},{72,8},{73,9},{16,80},{1... | collective-permute-start | bytes 221192 | tf_op jit(solution)/shard_map/ppermute | solution.py:39
where the time goes:
time: 159 us
  waiting for transfers between devices  87.6 us (55%)
  starting transfers between devices  47.5 us (30%)
  Pallas kernels  16.8 us (11%)
  local copies, waits for them, and re-layouts  3.25 us (2%)
  other arithmetic  2.89 us (2%)
    ppermute x35, waiting for transfers between devices, send(): return lax.ppermute(value, AXES, pairs)  87.6 us
    ppermute x35, starting transfers between devices, send(): return lax.ppermute(value, AXES, pairs)  47.5 us
    pallas_call x4, Pallas kernels, product(): pl.pallas_call(functools.partial(product_kernel, len(a), extra is not Non...  12 us
  transfers between devices with their start and end apart: 35, of which 20 were waited for; matrix products, arithmetic and copies ran while one was open for 3% of the time, Pallas kernels for 9%

commit v1 on v0

--- a/solution.py
+++ b/solution.py
@@ -99,49 +99,39 @@
     )(g, cosine, sine, swap, x, down_t, up)
 
 
-def product_kernel(chunks, adds, *refs):
+def product_kernel(chunks, keep, *refs):
     a_refs, b_refs, pieces = refs[:chunks], refs[chunks : 2 * chunks], refs[2 * chunks :]
-    out_refs = refs[-2:] if adds else refs[-1:]
+    out_refs = refs[-2:]
     _, y, _, x, k = place()
-    core = k if adds else 1 - k
-    block = 512
-    rows = block * 2
+    core = k if keep else 1 - k
+    block = out_refs[0].shape[1]
     each = a_refs[0].shape[0] // block
-    for i in range(rows // block):
+    for i in range(2):
         at = pl.ds((i % each) * block, block)
         left = jnp.concatenate([a_refs[i // each][at, :], b_refs[i // each][at, :]], axis=1)
         for r in range(4):
             if r == 2:
-                from_prev, from_next = pieces[4], pieces[5]
-                kept = jnp.concatenate([from_prev[0, core], from_next[0, core]], axis=0)
-                other = jnp.concatenate([from_prev[1, core], from_next[1, core]], axis=0)
+                kept = jnp.concatenate([pieces[4][core], pieces[5][core]], axis=0)
+                other = jnp.concatenate([pieces[6][core], pieces[7][core]], axis=0)
             else:
-                first = {0: 0, 1: 2, 3: 6}[r]
+                first = {0: 0, 1: 2, 3: 8}[r]
                 kept, other = pieces[first][core], pieces[first + 1][core]
             total = nt(left, jnp.concatenate([kept, other], axis=1))
             to = (y + r + 4 - x) % 4
-            if adds:
-                total = total + refs[-3][to, i * block : (i + 1) * block, :].astype(F32)
-                out_refs[i][to] = total.astype(BF16)
-            else:
-                out_refs[0][to, i * block : (i + 1) * block, :] = total.astype(BF16)
-
-
-def product(a, b, pieces, extra=None):
+            out_refs[i][to] = total.astype(out_refs[i].dtype)
+
+
+def product(a, b, pieces, keep):
     rows = sum(c.shape[0] for c in a)
     width = a[0].shape[1]
     cols = pieces[0].shape[1]
     args = [*a, *b, *pieces]
-    if extra is not None:
-        args.append(extra)
     vmem = pl.BlockSpec(memory_space=pltpu.VMEM)
     return pl.pallas_call(
-        functools.partial(product_kernel, len(a), extra is not None),
+        functools.partial(product_kernel, len(a), keep),
         in_specs=[vmem] * len(args),
-        out_specs=vmem if extra is None else [vmem] * 2,
-        out_shape=jax.ShapeDtypeStruct((4, rows, cols), BF16)
-        if extra is None
-        else [jax.ShapeDtypeStruct((4, rows // 2, cols), BF16)] * 2,
+        out_specs=[vmem] * 2,
+        out_shape=[jax.ShapeDtypeStruct((4, rows // 2, cols), F32 if keep else BF16)] * 2,
         compiler_params=pltpu.CompilerParams(vmem_limit_bytes=16 << 20),
         cost_estimate=pl.CostEstimate(
             flops=2 * rows * 2 * width * 4 * cols,
@@ -215,16 +205,41 @@
     )(own, own_moved, far_moved, near_moved, low, down_t)
 
 
-def reduce_over_x(top, low):
-    far_up = send(top[2], dx=1)
-    far_down = send(low[2], dx=-1)
-    up_low = send(low[1], dx=1)
-    down_top = send(top[3], dx=-1)
-    up_top = send((top[1].astype(F32) + far_up.astype(F32)).astype(BF16), dx=1)
-    down_low = send((low[3].astype(F32) + far_down.astype(F32)).astype(BF16), dx=-1)
-    first = top[0].astype(F32) + up_top.astype(F32) + down_top.astype(F32)
-    second = low[0].astype(F32) + up_low.astype(F32) + down_low.astype(F32)
-    return jnp.concatenate([first, second], axis=0)
+def add_up_kernel(*refs):
+    kept, arrived, ups, downs, out_ref = refs[:2], refs[2:4], refs[4:6], refs[6:8], refs[8]
+    rows = ups[0].shape[0]
+    for i in range(2):
+        total = kept[i][0] + arrived[i][0].astype(F32)
+        total = total + ups[i][...].astype(F32) + downs[i][...].astype(F32)
+        out_ref[i * rows : (i + 1) * rows, :] = total.astype(BF16)
+
+
+def add_up(kept, arrived, ups, downs):
+    rows, cols = ups[0].shape
+    vmem = pl.BlockSpec(memory_space=pltpu.VMEM)
+    return pl.pallas_call(
+        add_up_kernel,
+        in_specs=[vmem] * 8,
+        out_specs=vmem,
+        out_shape=jax.ShapeDtypeStruct((2 * rows, cols), BF16),
+        compiler_params=pltpu.CompilerParams(vmem_limit_bytes=14 << 20),
+        cost_estimate=pl.CostEstimate(
+            flops=8 * rows * cols, bytes_accessed=24 * rows * cols, transcendentals=0
+        ),
+    )(*kept, *arrived, *ups, *downs)
+
+
+def reduce_over_x(kept, arrived):
+    def term(to, low):
+        return kept[low][to] + arrived[low][to].astype(F32)
+
+    far_up = send(term(2, False).astype(BF16), dx=1)
+    far_down = send(term(2, True).astype(BF16), dx=-1)
+    up_low = send(term(1, True).astype(BF16), dx=1)
+    down_top = send(term(3, False).astype(BF16), dx=-1)
+    up_top = send((term(1, False) + far_up.astype(F32)).astype(BF16), dx=1)
+    down_low = send((term(3, True) + far_down.astype(F32)).astype(BF16), dx=-1)
+    return add_up(kept, arrived, (up_top, up_low), (down_top, down_low))
 
 
 def in_order(normed_input, positions, weight, down, up, gradient):
@@ -238,9 +253,9 @@
     half = kept.shape[1] // 2
     k_prev, k_next = send(kept, dy=1), send(kept, dy=-1)
     o_prev, o_next = send(other, dy=1), send(other, dy=-1)
-    far_prev = send(jnp.stack([k_prev[:, :half], o_prev[:, :half]]), dy=1)
-    far_next = send(jnp.stack([k_next[:, half:], o_next[:, half:]]), dy=-1)
-    pieces = (kept, other, k_next, o_next, far_prev, far_next, k_prev, o_prev)
+    k_far = send(k_prev[:, :half], dy=1), send(k_next[:, half:], dy=-1)
+    o_far = send(o_prev[:, :half], dy=1), send(o_next[:, half:], dy=-1)
+    pieces = (kept, other, k_next, o_next, *k_far, *o_far, k_prev, o_prev)
 
     lanes = jnp.arange(HEAD, dtype=jnp.int32)
     pair = (lanes // 2).astype(F32)
@@ -272,10 +287,10 @@
     for a, b in (([grad_y], [near]), ([far_top, far_low], [cross])):
         if len(a) != len(b):
             b = [b[0][:mid], b[0][mid:]]
-        partial = product(a, b, pieces)
-        arrived = send(partial, dk=1)
-        top, low_half = product(a, b, pieces, arrived)
-        sums.append(reduce_over_x(top, low_half).astype(BF16))
+        partial = product(a, b, pieces, False)
+        arrived = [send(p, dk=1) for p in partial]
+        total = product(a, b, pieces, True)
+        sums.append(reduce_over_x(total, arrived))
     own, opposite = sums
 
     own_moved = send(own, zmap={1: 0, 2: 3})

time: 159 us -> 150 us (0.943)
  the two profiles are of different devices: /device:TPU:32 before, /device:TPU:6 now
where the time goes in v1:
time: 150 us
  waiting for transfers between devices  71.6 us (48%)
  starting transfers between devices  54 us (36%)
  Pallas kernels  17.3 us (12%)
  local copies, waits for them, and re-layouts  3.1 us (2%)
  other arithmetic  2.81 us (2%)
    ppermute x39, waiting for transfers between devices, send(): return lax.ppermute(value, AXES, pairs)  71.6 us
    ppermute x39, starting transfers between devices, send(): return lax.ppermute(value, AXES, pairs)  54 us
    pallas_call x4, Pallas kernels, product(): pl.pallas_call(functools.partial(product_kernel, len(a), keep), in_specs=...  12.1 us
  transfers between devices with their start and end apart: 39, of which 19 were waited for; matrix products, arithmetic and copies ran while one was open for 3% of the time, Pallas kernels for 10%

profile of v1, /device:TPU:6, one launch (start us, length us, event | category | flops | bytes accessed | tf_op | source)
XLA Modules:
  0.0 149.9 jit_solution(18376876647742873641)
XLA Ops:
  0.7 1.6 %dynamic-slice_bitcast_fusion = (bf16[2,256,640]{2,1,0:T(8,128)(2,1)S(1)}, bf16[2,256,640]{2,1,0:T(8,128)(2,1)S(1)}) fusion(bf16[2,2,256,640]{3,2,1,0:T(8,128)(2,1)} %bitcast.46, s32[]{:T(128)S(6)} %select_n.51, s32[]{:T(128)S(6)} %select_n.50), kind=kLoop, calls=%fused_computation.2 | loop fusion | bytes 2621448 | tf_op jit(solution)/shard_map/jit(dynamic_index_in_dim)/squeeze | solution.py:251
  2.3 2.0 %collective-permute-start.1 = (bf16[2,256,640]{2,1,0:T(8,128)(2,1)S(1)}, bf16[2,256,640]{2,1,0:T(8,128)(2,1)S(1)}, u32[]{:S(2)}, u32[]{:S(2)}) collective-permute-start(bf16[2,256,640]{2,1,0:T(8,128)(2,1)S(1)} %get-tuple-element.37), channel_id=1, source_target_pairs={{0,8},{1,9},{8,0},{9,1},{64,72},{65,73},{72,64},{73,65},{16,24},{1... | collective-permute-start | bytes 1966088 | tf_op jit(solution)/shard_map/ppermute | solution.py:39
  4.3 1.6 %collective-permute-start.4 = (bf16[2,256,640]{2,1,0:T(8,128)(2,1)S(1)}, bf16[2,256,640]{2,1,0:T(8,128)(2,1)S(1)}, u32[]{:S(2)}, u32[]{:S(2)}) collective-permute-start(bf16[2,256,640]{2,1,0:T(8,128)(2,1)S(1)} %get-tuple-element.38.refs_2_.refs_4_), channel_id=1, source_target_pairs={{0,16},{1,17},{8,24},{9,25},{64,80},{65,81},{72,88},{73,89},{16,32... | collective-permute-start | bytes 1966088 | tf_op jit(solution)/shard_map/ppermute | solution.py:39
  5.9 1.9 %multiply_sine_fusion = (f32[1024,128]{1,0:T(8,128)S(1)}, f32[1024,128]{1,0:T(8,128)S(1)}) fusion(f32[128]{0:T(128)S(1)} %fusion.14, f32[1024]{0:T(1024)S(1)} %convert_element_type.133), kind=kLoop, calls=%fused_computation | loop fusion | flops 131072 | bytes 1053184 | tf_op jit(solution)/shard_map/sin | solution.py:266
  7.8 2.1 %shard_map.85 = (bf16[1024,640]{1,0:T(8,128)(2,1)S(1)}, f32[32,1024]{1,0:T(8,128)S(1)}) custom-call(bf16[1024,640]{1,0:T(8,128)(2,1)S(1)} %copy-done.1, f32[1024,128]{1,0:T(8,128)S(1)} %get-tuple-element.40.cos_ref, f32[1024,128]{1,0:T(8,128)S(1)} %get-tuple-element.39.sin_ref, bf16[128,128]{1,0:T(8,128)(2,1)S(1)} %select_convert_fusion.swap_ref, ...), custom_call_target="tpu_custom_call" | custom-call | flops 209715200 | bytes 5242880 | tf_op jit(solution)/shard_map/pallas_call | solution.py:76
  9.9 2.5 %collective-permute-start.19 = (bf16[1024,640]{1,0:T(8,128)(2,1)S(1)}, bf16[1024,640]{1,0:T(8,128)(2,1)S(1)}, u32[]{:S(2)}, u32[]{:S(2)}) collective-permute-start(bf16[1024,640]{1,0:T(8,128)(2,1)S(1)} %get-tuple-element.15.refs_0_.y_ref), channel_id=1, source_target_pairs={{0,72},{1,73},{8,64},{9,65},{64,8},{65,9},{72,0},{73,1},{16,88},{1... | collective-permute-start | bytes 3932168 | tf_op jit(solution)/shard_map/ppermute | solution.py:39
  13.5 1.7 %collective-permute-start.2 = (bf16[2,256,640]{2,1,0:T(8,128)(2,1)S(1)}, bf16[2,256,640]{2,1,0:T(8,128)(2,1)S(1)}, u32[]{:S(2)}, u32[]{:S(2)}) collective-permute-start(bf16[2,256,640]{2,1,0:T(8,128)(2,1)S(1)} %get-tuple-element.38.refs_2_.refs_4_), channel_id=1, source_target_pairs={{0,48},{1,49},{8,56},{9,57},{64,112},{65,113},{72,120},{73,121},{1... | collective-permute-start | bytes 1966088 | tf_op jit(solution)/shard_map/ppermute | solution.py:39
  15.1 4.8 %collective-permute-done.1.refs_3_.refs_5_ = bf16[2,256,640]{2,1,0:T(8,128)(2,1)S(1)} collective-permute-done((bf16[2,256,640]{2,1,0:T(8,128)(2,1)S(1)}, bf16[2,256,640]{2,1,0:T(8,128)(2,1)S(1)}, u32[]{:S(2)}, u32[]{:S(2)}) %collective-permute-start.1) | collective-permute-done | bytes 655392 | tf_op jit(solution)/shard_map/ppermute | solution.py:39
  20.0 1.6 %collective-permute-start.7 = (bf16[2,256,640]{2,1,0:T(8,128)(2,1)S(1)}, bf16[2,256,640]{2,1,0:T(8,128)(2,1)S(1)}, u32[]{:S(2)}, u32[]{:S(2)}) collective-permute-start(bf16[2,256,640]{2,1,0:T(8,128)(2,1)S(1)} %collective-permute-done.1.refs_3_.refs_5_), channel_id=1, source_target_pairs={{0,16},{1,17},{8,24},{9,25},{64,80},{65,81},{72,88},{73,89},{16,32... | collective-permute-start | bytes 1966088 | tf_op jit(solution)/shard_map/ppermute | solution.py:39
  21.7 1.7 %collective-permute-start.3 = (bf16[2,256,640]{2,1,0:T(8,128)(2,1)S(1)}, bf16[2,256,640]{2,1,0:T(8,128)(2,1)S(1)}, u32[]{:S(2)}, u32[]{:S(2)}) collective-permute-start(bf16[2,256,640]{2,1,0:T(8,128)(2,1)S(1)} %collective-permute-done.1.refs_3_.refs_5_), channel_id=1, source_target_pairs={{0,48},{1,49},{8,56},{9,57},{64,112},{65,113},{72,120},{73,121},{1... | collective-permute-start | bytes 1966088 | tf_op jit(solution)/shard_map/ppermute | solution.py:39
  23.5 7.6 %collective-permute-done.2.refs_4_.refs_6_ = bf16[2,256,640]{2,1,0:T(8,128)(2,1)S(1)} collective-permute-done((bf16[2,256,640]{2,1,0:T(8,128)(2,1)S(1)}, bf16[2,256,640]{2,1,0:T(8,128)(2,1)S(1)}, u32[]{:S(2)}, u32[]{:S(2)}) %collective-permute-start.2) | collective-permute-done | bytes 655392 | tf_op jit(solution)/shard_map/ppermute | solution.py:39
  31.1 1.6 %collective-permute-start.5 = (bf16[2,128,640]{2,1,0:T(8,128)(2,1)S(1)}, bf16[2,128,640]{2,1,0:T(8,128)(2,1)S(1)}, u32[]{:S(2)}, u32[]{:S(2)}) collective-permute-start(bf16[2,128,640]{2,1,0:T(8,128)(2,1)S(1)} %slice.133), channel_id=1, source_target_pairs={{0,16},{1,17},{8,24},{9,25},{64,80},{65,81},{72,88},{73,89},{16,32... | collective-permute-start | bytes 983048 | tf_op jit(solution)/shard_map/ppermute | solution.py:39
  32.7 6.1 %collective-permute-done.7.refs_11_.refs_13_ = bf16[2,256,640]{2,1,0:T(8,128)(2,1)S(1)} collective-permute-done((bf16[2,256,640]{2,1,0:T(8,128)(2,1)S(1)}, bf16[2,256,640]{2,1,0:T(8,128)(2,1)S(1)}, u32[]{:S(2)}, u32[]{:S(2)}) %collective-permute-start.7) | collective-permute-done | bytes 655392 | tf_op jit(solution)/shard_map/ppermute | solution.py:39
  38.8 1.8 %collective-permute-start.6 = (bf16[2,128,640]{2,1,0:T(8,128)(2,1)S(1)}, bf16[2,128,640]{2,1,0:T(8,128)(2,1)S(1)}, u32[]{:S(2)}, u32[]{:S(2)}) collective-permute-start(bf16[2,128,640]{2,1,0:T(8,128)(2,1)S(1)} %slice.134), channel_id=1, source_target_pairs={{0,48},{1,49},{8,56},{9,57},{64,112},{65,113},{72,120},{73,121},{1... | collective-permute-start | bytes 983048 | tf_op jit(solution)/shard_map/ppermute | solution.py:39
  40.6 4.5 %collective-permute-done.3.refs_5_.refs_7_ = bf16[2,256,640]{2,1,0:T(8,128)(2,1)S(1)} collective-permute-done((bf16[2,256,640]{2,1,0:T(8,128)(2,1)S(1)}, bf16[2,256,640]{2,1,0:T(8,128)(2,1)S(1)}, u32[]{:S(2)}, u32[]{:S(2)}) %collective-permute-start.3) | collective-permute-done | bytes 655392 | tf_op jit(solution)/shard_map/ppermute | solution.py:39
  45.1 1.6 %collective-permute-start.8 = (bf16[2,128,640]{2,1,0:T(8,128)(2,1)S(1)}, bf16[2,128,640]{2,1,0:T(8,128)(2,1)S(1)}, u32[]{:S(2)}, u32[]{:S(2)}) collective-permute-start(bf16[2,128,640]{2,1,0:T(8,128)(2,1)S(1)} %slice.135), channel_id=1, source_target_pairs={{0,16},{1,17},{8,24},{9,25},{64,80},{65,81},{72,88},{73,89},{16,32... | collective-permute-start | bytes 983048 | tf_op jit(solution)/shard_map/ppermute | solution.py:39
  46.8 1.7 %collective-permute-start.9 = (bf16[2,128,640]{2,1,0:T(8,128)(2,1)S(1)}, bf16[2,128,640]{2,1,0:T(8,128)(2,1)S(1)}, u32[]{:S(2)}, u32[]{:S(2)}) collective-permute-start(bf16[2,128,640]{2,1,0:T(8,128)(2,1)S(1)} %slice.136), channel_id=1, source_target_pairs={{0,48},{1,49},{8,56},{9,57},{64,112},{65,113},{72,120},{73,121},{1... | collective-permute-start | bytes 983048 | tf_op jit(solution)/shard_map/ppermute | solution.py:39
  48.6 1.1 collective-permute-start.20
  49.8 1.7 %collective-permute-start.21 = (bf16[512,640]{1,0:T(8,128)(2,1)S(1)}, bf16[512,640]{1,0:T(8,128)(2,1)S(1)}, u32[]{:S(2)}, u32[]{:S(2)}) collective-permute-start(bf16[512,640]{1,0:T(8,128)(2,1)S(1)} %slice.144), channel_id=1, source_target_pairs={{0,72},{1,73},{8,64},{9,65},{64,8},{65,9},{72,0},{73,1},{16,88},{1... | collective-permute-start | bytes 1966088 | tf_op jit(solution)/shard_map/ppermute | solution.py:39
  52.2 1.3 collective-permute-done.8.refs_8_.refs_10_
  53.4 3.5 %collective-permute-done.9.refs_9_.refs_11_ = bf16[2,128,640]{2,1,0:T(8,128)(2,1)S(1)} collective-permute-done((bf16[2,128,640]{2,1,0:T(8,128)(2,1)S(1)}, bf16[2,128,640]{2,1,0:T(8,128)(2,1)S(1)}, u32[]{:S(2)}, u32[]{:S(2)}) %collective-permute-start.9) | collective-permute-done | bytes 327712 | tf_op jit(solution)/shard_map/ppermute | solution.py:39
  56.9 3.0 %shard_map.87 = (bf16[4,512,256]{2,1,0:T(8,128)(2,1)S(1)}, bf16[4,512,256]{2,1,0:T(8,128)(2,1)S(1)}) custom-call(bf16[1024,640]{1,0:T(8,128)(2,1)S(1)} %get-tuple-element.15.refs_0_.y_ref, bf16[1024,640]{1,0:T(8,128)(2,1)S(1)} %collective-permute-done.refs_1_, bf16[2,256,640]{2,1,0:T(8,128)(2,1)S(1)} %get-tuple-element.38.refs_2_.refs_4_, ...), custom_call_target="tpu_custom_call" | custom-call | flops 2684354560 | bytes 7340032 | tf_op jit(solution)/shard_map/pallas_call | solution.py:130
  60.0 1.1 collective-permute-start.32
  61.1 4.8 %collective-permute-done.32 = f32[32,1024]{1,0:T(8,128)S(1)} collective-permute-done((f32[32,1024]{1,0:T(8,128)S(1)}, f32[32,1024]{1,0:T(8,128)S(1)}, u32[]{:S(2)}, u32[]{:S(2)}) %collective-permute-start.32) | collective-permute-done | bytes 131104 | tf_op jit(solution)/shard_map/ppermute | solution.py:39
  67.4 1.1 collective-permute-start.34
  68.5 3.0 %shard_map.90 = (bf16[4,512,256]{2,1,0:T(8,128)(2,1)S(1)}, bf16[4,512,256]{2,1,0:T(8,128)(2,1)S(1)}) custom-call(bf16[512,640]{1,0:T(8,128)(2,1)S(1)} %collective-permute-done.20.refs_0_, bf16[512,640]{1,0:T(8,128)(2,1)S(1)} %collective-permute-done.21.refs_1_, bf16[512,640]{1,0:T(8,128)(2,1)S(1)} %get-tuple-element.36.refs_2_, ...), custom_call_target="tpu_custom_call" | custom-call | flops 2684354560 | bytes 7340032 | tf_op jit(solution)/shard_map/pallas_call | solution.py:130
  71.6 3.1 %shard_map.86 = (f32[4,512,256]{2,1,0:T(8,128)S(1)}, f32[4,512,256]{2,1,0:T(8,128)S(1)}) custom-call(bf16[1024,640]{1,0:T(8,128)(2,1)S(1)} %get-tuple-element.15.refs_0_.y_ref, bf16[1024,640]{1,0:T(8,128)(2,1)S(1)} %collective-permute-done.refs_1_, bf16[2,256,640]{2,1,0:T(8,128)(2,1)S(1)} %get-tuple-element.38.refs_2_.refs_4_, ...), custom_call_target="tpu_custom_call" | custom-call | flops 2684354560 | bytes 7340032 | tf_op jit(solution)/shard_map/pallas_call | solution.py:130
  75.3 1.2 collective-permute-start.12
  76.5 3.1 %shard_map.89 = (f32[4,512,256]{2,1,0:T(8,128)S(1)}, f32[4,512,256]{2,1,0:T(8,128)S(1)}) custom-call(bf16[512,640]{1,0:T(8,128)(2,1)S(1)} %collective-permute-done.20.refs_0_, bf16[512,640]{1,0:T(8,128)(2,1)S(1)} %collective-permute-done.21.refs_1_, bf16[512,640]{1,0:T(8,128)(2,1)S(1)} %get-tuple-element.36.refs_2_, ...), custom_call_target="tpu_custom_call" | custom-call | flops 2684354560 | bytes 7340032 | tf_op jit(solution)/shard_map/pallas_call | solution.py:130
  80.4 4.2 %collective-permute-done.12 = bf16[512,256]{1,0:T(8,128)(2,1)S(1)} collective-permute-done((bf16[512,256]{1,0:T(8,128)(2,1)S(1)}, bf16[512,256]{1,0:T(8,128)(2,1)S(1)}, u32[]{:S(2)}, u32[]{:S(2)}) %collective-permute-start.12) | collective-permute-done | bytes 262176 | tf_op jit(solution)/shard_map/ppermute | solution.py:39
  84.6 1.2 collective-permute-start.15
  86.1 3.3 %collective-permute-start.24 = (bf16[512,256]{1,0:T(8,128)(2,1)S(1)}, bf16[512,256]{1,0:T(8,128)(2,1)S(1)}, u32[]{:S(2)}, u32[]{:S(2)}) collective-permute-start(bf16[512,256]{1,0:T(8,128)(2,1)S(1)} %get-tuple-element.30), channel_id=1, source_target_pairs={{0,2},{1,3},{8,10},{9,11},{64,66},{65,67},{72,74},{73,75},{16,18},... | collective-permute-start | bytes 786440 | tf_op jit(solution)/shard_map/ppermute | solution.py:39
  89.5 8.4 %collective-permute-done.16 = bf16[512,256]{1,0:T(8,128)(2,1)S(1)} collective-permute-done((bf16[512,256]{1,0:T(8,128)(2,1)S(1)}, bf16[512,256]{1,0:T(8,128)(2,1)S(1)}, u32[]{:S(2)}, u32[]{:S(2)}) %collective-permute-start.16) | collective-permute-done | bytes 262176 | tf_op jit(solution)/shard_map/ppermute | solution.py:39
  98.0 3.3 %collective-permute-start.13 = (bf16[512,256]{1,0:T(8,128)(2,1)S(1)}, bf16[512,256]{1,0:T(8,128)(2,1)S(1)}, u32[]{:S(2)}, u32[]{:S(2)}) collective-permute-start(bf16[512,256]{1,0:T(8,128)(2,1)S(1)} %fusion.3), channel_id=1, source_target_pairs={{0,2},{1,3},{8,10},{9,11},{64,66},{65,67},{72,74},{73,75},{16,18},... | collective-permute-start | bytes 786440 | tf_op jit(solution)/shard_map/ppermute | solution.py:39
  101.4 4.1 %collective-permute-done.28 = bf16[512,256]{1,0:T(8,128)(2,1)S(1)} collective-permute-done((bf16[512,256]{1,0:T(8,128)(2,1)S(1)}, bf16[512,256]{1,0:T(8,128)(2,1)S(1)}, u32[]{:S(2)}, u32[]{:S(2)}) %collective-permute-start.28) | collective-permute-done | bytes 262176 | tf_op jit(solution)/shard_map/ppermute | solution.py:39
  105.6 3.3 %collective-permute-start.26 = (bf16[512,256]{1,0:T(8,128)(2,1)S(1)}, bf16[512,256]{1,0:T(8,128)(2,1)S(1)}, u32[]{:S(2)}, u32[]{:S(2)}) collective-permute-start(bf16[512,256]{1,0:T(8,128)(2,1)S(1)} %get-tuple-element.28), channel_id=1, source_target_pairs={{0,2},{1,3},{8,10},{9,11},{64,66},{65,67},{72,74},{73,75},{16,18},... | collective-permute-start | bytes 786440 | tf_op jit(solution)/shard_map/ppermute | solution.py:39
  108.9 3.2 %collective-permute-start.25 = (bf16[512,256]{1,0:T(8,128)(2,1)S(1)}, bf16[512,256]{1,0:T(8,128)(2,1)S(1)}, u32[]{:S(2)}, u32[]{:S(2)}) collective-permute-start(bf16[512,256]{1,0:T(8,128)(2,1)S(1)} %fusion.1), channel_id=1, source_target_pairs={{0,2},{1,3},{8,10},{9,11},{64,66},{65,67},{72,74},{73,75},{16,18},... | collective-permute-start | bytes 786440 | tf_op jit(solution)/shard_map/ppermute | solution.py:39
  112.2 3.7 %collective-permute-done.17.refs_7_ = bf16[512,256]{1,0:T(8,128)(2,1)S(1)} collective-permute-done((bf16[512,256]{1,0:T(8,128)(2,1)S(1)}, bf16[512,256]{1,0:T(8,128)(2,1)S(1)}, u32[]{:S(2)}, u32[]{:S(2)}) %collective-permute-start.17) | collective-permute-done | bytes 262176 | tf_op jit(solution)/shard_map/ppermute | solution.py:39
  116.1 1.3 collective-permute-start.18
  117.4 3.6 %collective-permute-done.27.refs_6_ = bf16[512,256]{1,0:T(8,128)(2,1)S(1)} collective-permute-done((bf16[512,256]{1,0:T(8,128)(2,1)S(1)}, bf16[512,256]{1,0:T(8,128)(2,1)S(1)}, u32[]{:S(2)}, u32[]{:S(2)}) %collective-permute-start.27) | collective-permute-done | bytes 262176 | tf_op jit(solution)/shard_map/ppermute | solution.py:39
  121.1 2.8 %collective-permute-done.29.refs_7_ = bf16[512,256]{1,0:T(8,128)(2,1)S(1)} collective-permute-done((bf16[512,256]{1,0:T(8,128)(2,1)S(1)}, bf16[512,256]{1,0:T(8,128)(2,1)S(1)}, u32[]{:S(2)}, u32[]{:S(2)}) %collective-permute-start.29) | collective-permute-done | bytes 262176 | tf_op jit(solution)/shard_map/ppermute | solution.py:39
  124.1 5.1 %collective-permute-start.30 = (bf16[1024,256]{1,0:T(8,128)(2,1)S(1)}, bf16[1024,256]{1,0:T(8,128)(2,1)S(1)}, u32[]{:S(2)}, u32[]{:S(2)}) collective-permute-start(bf16[1024,256]{1,0:T(8,128)(2,1)S(1)} %shard_map.91), channel_id=1, source_target_pairs={{0,64},{1,65},{72,8},{73,9},{16,80},{17,81},{88,24},{89,25},{32,96... | collective-permute-start | bytes 1572872 | tf_op jit(solution)/shard_map/ppermute | solution.py:39
  130.4 1.6 %collective-permute-start.36 = (f32[16,1152]{1,0:T(8,128)S(1)}, f32[16,1152]{1,0:T(8,128)S(1)}, u32[]{:S(2)}, u32[]{:S(2)}) collective-permute-start(f32[16,1152]{1,0:T(8,128)S(1)} %get-tuple-element.26), channel_id=1, source_target_pairs={{0,16},{1,17},{8,24},{9,25},{64,80},{65,81},{72,88},{73,89},{16,0}... | collective-permute-start | bytes 221192 | tf_op jit(solution)/shard_map/ppermute | solution.py:39
  132.0 2.8 %collective-permute-done.36 = f32[16,1152]{1,0:T(8,128)S(1)} collective-permute-done((f32[16,1152]{1,0:T(8,128)S(1)}, f32[16,1152]{1,0:T(8,128)S(1)}, u32[]{:S(2)}, u32[]{:S(2)}) %collective-permute-start.36) | collective-permute-done | bytes 73760 | tf_op jit(solution)/shard_map/ppermute | solution.py:39
  134.8 3.1 %collective-permute-start.37 = (f32[16,1152]{1,0:T(8,128)S(1)}, f32[16,1152]{1,0:T(8,128)S(1)}, u32[]{:S(2)}, u32[]{:S(2)}) collective-permute-start(f32[16,1152]{1,0:T(8,128)S(1)} %add.137), channel_id=1, source_target_pairs={{0,48},{1,49},{8,56},{9,57},{64,112},{65,113},{72,120},{73,121},{1... | collective-permute-start | bytes 221192 | tf_op jit(solution)/shard_map/ppermute | solution.py:39
  137.9 2.6 %collective-permute-done.37 = f32[16,1152]{1,0:T(8,128)S(1)} collective-permute-done((f32[16,1152]{1,0:T(8,128)S(1)}, f32[16,1152]{1,0:T(8,128)S(1)}, u32[]{:S(2)}, u32[]{:S(2)}) %collective-permute-start.37) | collective-permute-done | bytes 73760 | tf_op jit(solution)/shard_map/ppermute | solution.py:39
  141.3 5.1 %collective-permute-done.38 = f32[16,1152]{1,0:T(8,128)S(1)} collective-permute-done((f32[16,1152]{1,0:T(8,128)S(1)}, f32[16,1152]{1,0:T(8,128)S(1)}, u32[]{:S(2)}, u32[]{:S(2)}) %collective-permute-start.38) | collective-permute-done | bytes 73760 | tf_op jit(solution)/shard_map/ppermute | solution.py:39
  147.7 2.2 %shard_map.93 = bf16[1024,512]{1,0:T(8,128)(2,1)} custom-call(bf16[1024,256]{1,0:T(8,128)(2,1)S(1)} %shard_map.88.own_ref, bf16[1024,256]{1,0:T(8,128)(2,1)S(1)} %collective-permute-done.18.own_moved_ref, bf16[1024,256]{1,0:T(8,128)(2,1)S(1)} %collective-permute-done.30.far_moved_ref, bf16[1024,256]{1,0:T(8,128)(2,1)S(1)} %collective-permute-done.31.near_moved_ref, ...), custom_call_target="tpu_custom_call" | custom-call | flops 16777216 | bytes 3145728 | tf_op jit(solution)/shard_map/pallas_call | solution.py:189
  (78 shorter events, 9.7 us)
Async XLA Ops:
  0.6 5.2 %copy-start.4 = (s32[1024]{0:T(1024)S(1)}, s32[1024]{0:T(1024)}, u32[]{:S(2)}) copy-start(s32[1024]{0:T(1024)} %param.7) | copy-start | bytes 12292
  0.6 7.2 %copy-start.1 = (bf16[1024,640]{1,0:T(8,128)(2,1)S(1)}, bf16[1024,640]{1,0:T(8,128)(2,1)}, u32[]{:S(2)}) copy-start(bf16[1024,640]{1,0:T(8,128)(2,1)} %g_ref.1) | copy-start | bytes 3932164
  0.7 7.2 %copy-start = (bf16[1024,512]{1,0:T(8,128)(2,1)S(1)}, bf16[1024,512]{1,0:T(8,128)(2,1)}, u32[]{:S(2)}) copy-start(bf16[1024,512]{1,0:T(8,128)(2,1)} %x_ref.3) | copy-start | bytes 3145732
  0.7 7.2 %copy-start.2 = (bf16[512,16]{0,1:T(8,128)(2,1)S(1)}, bf16[512,16]{0,1:T(8,128)(2,1)}, u32[]{:S(2)}) copy-start(bf16[512,16]{0,1:T(8,128)(2,1)} %param.9) | copy-start | bytes 49156
  0.7 7.2 %copy-start.3 = (bf16[16,640]{1,0:T(8,128)(2,1)S(1)}, bf16[16,640]{1,0:T(8,128)(2,1)}, u32[]{:S(2)}) copy-start(bf16[16,640]{1,0:T(8,128)(2,1)} %up_ref.1) | copy-start | bytes 61444
  2.3 17.7 %collective-permute-start.1 = (bf16[2,256,640]{2,1,0:T(8,128)(2,1)S(1)}, bf16[2,256,640]{2,1,0:T(8,128)(2,1)S(1)}, u32[]{:S(2)}, u32[]{:S(2)}) collective-permute-start(bf16[2,256,640]{2,1,0:T(8,128)(2,1)S(1)} %get-tuple-element.37), channel_id=1, source_target_pairs={{0,8},{1,9},{8,0},{9,1},{64,72},{65,73},{72,64},{73,65},{16,24},{1... | collective-permute-start | bytes 1966088 | tf_op jit(solution)/shard_map/ppermute | solution.py:39
  4.3 17.5 %collective-permute-start.4 = (bf16[2,256,640]{2,1,0:T(8,128)(2,1)S(1)}, bf16[2,256,640]{2,1,0:T(8,128)(2,1)S(1)}, u32[]{:S(2)}, u32[]{:S(2)}) collective-permute-start(bf16[2,256,640]{2,1,0:T(8,128)(2,1)S(1)} %get-tuple-element.38.refs_2_.refs_4_), channel_id=1, source_target_pairs={{0,16},{1,17},{8,24},{9,25},{64,80},{65,81},{72,88},{73,89},{16,32... | collective-permute-start | bytes 1966088 | tf_op jit(solution)/shard_map/ppermute | solution.py:39
  9.9 36.8 %collective-permute-start.19 = (bf16[1024,640]{1,0:T(8,128)(2,1)S(1)}, bf16[1024,640]{1,0:T(8,128)(2,1)S(1)}, u32[]{:S(2)}, u32[]{:S(2)}) collective-permute-start(bf16[1024,640]{1,0:T(8,128)(2,1)S(1)} %get-tuple-element.15.refs_0_.y_ref), channel_id=1, source_target_pairs={{0,72},{1,73},{8,64},{9,65},{64,8},{65,9},{72,0},{73,1},{16,88},{1... | collective-permute-start | bytes 3932168 | tf_op jit(solution)/shard_map/ppermute | solution.py:39
  12.5 36.1 %collective-permute-start = (bf16[1024,640]{1,0:T(8,128)(2,1)S(1)}, bf16[1024,640]{1,0:T(8,128)(2,1)S(1)}, u32[]{:S(2)}, u32[]{:S(2)}) collective-permute-start(bf16[1024,640]{1,0:T(8,128)(2,1)S(1)} %get-tuple-element.15.refs_0_.y_ref), channel_id=1, source_target_pairs={{0,8},{1,9},{8,0},{9,1},{64,72},{65,73},{72,64},{73,65},{16,24},{1... | collective-permute-start | bytes 3932168 | tf_op jit(solution)/shard_map/ppermute | solution.py:39
  13.5 17.6 %collective-permute-start.2 = (bf16[2,256,640]{2,1,0:T(8,128)(2,1)S(1)}, bf16[2,256,640]{2,1,0:T(8,128)(2,1)S(1)}, u32[]{:S(2)}, u32[]{:S(2)}) collective-permute-start(bf16[2,256,640]{2,1,0:T(8,128)(2,1)S(1)} %get-tuple-element.38.refs_2_.refs_4_), channel_id=1, source_target_pairs={{0,48},{1,49},{8,56},{9,57},{64,112},{65,113},{72,120},{73,121},{1... | collective-permute-start | bytes 1966088 | tf_op jit(solution)/shard_map/ppermute | solution.py:39
  20.0 18.8 %collective-permute-start.7 = (bf16[2,256,640]{2,1,0:T(8,128)(2,1)S(1)}, bf16[2,256,640]{2,1,0:T(8,128)(2,1)S(1)}, u32[]{:S(2)}, u32[]{:S(2)}) collective-permute-start(bf16[2,256,640]{2,1,0:T(8,128)(2,1)S(1)} %collective-permute-done.1.refs_3_.refs_5_), channel_id=1, source_target_pairs={{0,16},{1,17},{8,24},{9,25},{64,80},{65,81},{72,88},{73,89},{16,32... | collective-permute-start | bytes 1966088 | tf_op jit(solution)/shard_map/ppermute | solution.py:39
  21.7 23.4 %collective-permute-start.3 = (bf16[2,256,640]{2,1,0:T(8,128)(2,1)S(1)}, bf16[2,256,640]{2,1,0:T(8,128)(2,1)S(1)}, u32[]{:S(2)}, u32[]{:S(2)}) collective-permute-start(bf16[2,256,640]{2,1,0:T(8,128)(2,1)S(1)} %collective-permute-done.1.refs_3_.refs_5_), channel_id=1, source_target_pairs={{0,48},{1,49},{8,56},{9,57},{64,112},{65,113},{72,120},{73,121},{1... | collective-permute-start | bytes 1966088 | tf_op jit(solution)/shard_map/ppermute | solution.py:39
  31.1 18.7 %collective-permute-start.5 = (bf16[2,128,640]{2,1,0:T(8,128)(2,1)S(1)}, bf16[2,128,640]{2,1,0:T(8,128)(2,1)S(1)}, u32[]{:S(2)}, u32[]{:S(2)}) collective-permute-start(bf16[2,128,640]{2,1,0:T(8,128)(2,1)S(1)} %slice.133), channel_id=1, source_target_pairs={{0,16},{1,17},{8,24},{9,25},{64,80},{65,81},{72,88},{73,89},{16,32... | collective-permute-start | bytes 983048 | tf_op jit(solution)/shard_map/ppermute | solution.py:39
  38.8 13.4 %collective-permute-start.6 = (bf16[2,128,640]{2,1,0:T(8,128)(2,1)S(1)}, bf16[2,128,640]{2,1,0:T(8,128)(2,1)S(1)}, u32[]{:S(2)}, u32[]{:S(2)}) collective-permute-start(bf16[2,128,640]{2,1,0:T(8,128)(2,1)S(1)} %slice.134), channel_id=1, source_target_pairs={{0,48},{1,49},{8,56},{9,57},{64,112},{65,113},{72,120},{73,121},{1... | collective-permute-start | bytes 983048 | tf_op jit(solution)/shard_map/ppermute | solution.py:39
  45.1 8.3 %collective-permute-start.8 = (bf16[2,128,640]{2,1,0:T(8,128)(2,1)S(1)}, bf16[2,128,640]{2,1,0:T(8,128)(2,1)S(1)}, u32[]{:S(2)}, u32[]{:S(2)}) collective-permute-start(bf16[2,128,640]{2,1,0:T(8,128)(2,1)S(1)} %slice.135), channel_id=1, source_target_pairs={{0,16},{1,17},{8,24},{9,25},{64,80},{65,81},{72,88},{73,89},{16,32... | collective-permute-start | bytes 983048 | tf_op jit(solution)/shard_map/ppermute | solution.py:39
  46.8 10.2 %collective-permute-start.9 = (bf16[2,128,640]{2,1,0:T(8,128)(2,1)S(1)}, bf16[2,128,640]{2,1,0:T(8,128)(2,1)S(1)}, u32[]{:S(2)}, u32[]{:S(2)}) collective-permute-start(bf16[2,128,640]{2,1,0:T(8,128)(2,1)S(1)} %slice.136), channel_id=1, source_target_pairs={{0,48},{1,49},{8,56},{9,57},{64,112},{65,113},{72,120},{73,121},{1... | collective-permute-start | bytes 983048 | tf_op jit(solution)/shard_map/ppermute | solution.py:39
  48.6 19.9 %collective-permute-start.20 = (bf16[512,640]{1,0:T(8,128)(2,1)S(1)}, bf16[512,640]{1,0:T(8,128)(2,1)S(1)}, u32[]{:S(2)}, u32[]{:S(2)}) collective-permute-start(bf16[512,640]{1,0:T(8,128)(2,1)S(1)} %get-tuple-element.36.refs_2_), channel_id=1, source_target_pairs={{0,8},{1,9},{8,0},{9,1},{64,72},{65,73},{72,64},{73,65},{16,24},{1... | collective-permute-start | bytes 1966088 | tf_op jit(solution)/shard_map/ppermute | solution.py:39
  49.8 18.7 %collective-permute-start.21 = (bf16[512,640]{1,0:T(8,128)(2,1)S(1)}, bf16[512,640]{1,0:T(8,128)(2,1)S(1)}, u32[]{:S(2)}, u32[]{:S(2)}) collective-permute-start(bf16[512,640]{1,0:T(8,128)(2,1)S(1)} %slice.144), channel_id=1, source_target_pairs={{0,72},{1,73},{8,64},{9,65},{64,8},{65,9},{72,0},{73,1},{16,88},{1... | collective-permute-start | bytes 1966088 | tf_op jit(solution)/shard_map/ppermute | solution.py:39
  59.9 15.3 %collective-permute-start.10 = (bf16[4,512,256]{2,1,0:T(8,128)(2,1)S(1)}, bf16[4,512,256]{2,1,0:T(8,128)(2,1)S(1)}, u32[]{:S(2)}, u32[]{:S(2)}) collective-permute-start(bf16[4,512,256]{2,1,0:T(8,128)(2,1)S(1)} %get-tuple-element.18), channel_id=1, source_target_pairs={{0,1},{1,0},{8,9},{9,8},{64,65},{65,64},{72,73},{73,72},{16,17},{1... | collective-permute-start | bytes 3145736 | tf_op jit(solution)/shard_map/ppermute | solution.py:39
  60.0 5.9 %collective-permute-start.32 = (f32[32,1024]{1,0:T(8,128)S(1)}, f32[32,1024]{1,0:T(8,128)S(1)}, u32[]{:S(2)}, u32[]{:S(2)}) collective-permute-start(f32[32,1024]{1,0:T(8,128)S(1)} %get-tuple-element.24), channel_id=1, source_target_pairs={{0,8},{1,9},{8,0},{9,1},{64,72},{65,73},{72,64},{73,65},{16,24},{1... | collective-permute-start | bytes 393224 | tf_op jit(solution)/shard_map/ppermute | solution.py:39
  65.9 1.4 collective-permute-start.33
  66.0 13.6 %collective-permute-start.11 = (bf16[4,512,256]{2,1,0:T(8,128)(2,1)S(1)}, bf16[4,512,256]{2,1,0:T(8,128)(2,1)S(1)}, u32[]{:S(2)}, u32[]{:S(2)}) collective-permute-start(bf16[4,512,256]{2,1,0:T(8,128)(2,1)S(1)} %get-tuple-element.19), channel_id=1, source_target_pairs={{0,1},{1,0},{8,9},{9,8},{64,65},{65,64},{72,73},{73,72},{16,17},{1... | collective-permute-start | bytes 3145736 | tf_op jit(solution)/shard_map/ppermute | solution.py:39
  67.4 38.2 %collective-permute-start.34 = (f32[32,1024]{1,0:T(8,128)S(1)}, f32[32,1024]{1,0:T(8,128)S(1)}, u32[]{:S(2)}, u32[]{:S(2)}) collective-permute-start(f32[32,1024]{1,0:T(8,128)S(1)} %add.135), channel_id=1, source_target_pairs={{0,2},{1,3},{8,10},{9,11},{64,66},{65,67},{72,74},{73,75},{16,18},... | collective-permute-start | bytes 393224 | tf_op jit(solution)/shard_map/ppermute | solution.py:39
  71.5 14.4 %collective-permute-start.22 = (bf16[4,512,256]{2,1,0:T(8,128)(2,1)S(1)}, bf16[4,512,256]{2,1,0:T(8,128)(2,1)S(1)}, u32[]{:S(2)}, u32[]{:S(2)}) collective-permute-start(bf16[4,512,256]{2,1,0:T(8,128)(2,1)S(1)} %get-tuple-element.22), channel_id=1, source_target_pairs={{0,1},{1,0},{8,9},{9,8},{64,65},{65,64},{72,73},{73,72},{16,17},{1... | collective-permute-start | bytes 3145736 | tf_op jit(solution)/shard_map/ppermute | solution.py:39
  74.7 11.4 %collective-permute-start.23 = (bf16[4,512,256]{2,1,0:T(8,128)(2,1)S(1)}, bf16[4,512,256]{2,1,0:T(8,128)(2,1)S(1)}, u32[]{:S(2)}, u32[]{:S(2)}) collective-permute-start(bf16[4,512,256]{2,1,0:T(8,128)(2,1)S(1)} %get-tuple-element.23), channel_id=1, source_target_pairs={{0,1},{1,0},{8,9},{9,8},{64,65},{65,64},{72,73},{73,72},{16,17},{1... | collective-permute-start | bytes 3145736 | tf_op jit(solution)/shard_map/ppermute | solution.py:39
  75.3 9.2 %collective-permute-start.12 = (bf16[512,256]{1,0:T(8,128)(2,1)S(1)}, bf16[512,256]{1,0:T(8,128)(2,1)S(1)}, u32[]{:S(2)}, u32[]{:S(2)}) collective-permute-start(bf16[512,256]{1,0:T(8,128)(2,1)S(1)} %get-tuple-element.34), channel_id=1, source_target_pairs={{0,2},{1,3},{8,10},{9,11},{64,66},{65,67},{72,74},{73,75},{16,18},... | collective-permute-start | bytes 786440 | tf_op jit(solution)/shard_map/ppermute | solution.py:39
  79.7 29.2 %collective-permute-start.14 = (bf16[512,256]{1,0:T(8,128)(2,1)S(1)}, bf16[512,256]{1,0:T(8,128)(2,1)S(1)}, u32[]{:S(2)}, u32[]{:S(2)}) collective-permute-start(bf16[512,256]{1,0:T(8,128)(2,1)S(1)} %get-tuple-element.32), channel_id=1, source_target_pairs={{0,2},{1,3},{8,10},{9,11},{64,66},{65,67},{72,74},{73,75},{16,18},... | collective-permute-start | bytes 786440 | tf_op jit(solution)/shard_map/ppermute | solution.py:39
  84.6 24.3 %collective-permute-start.15 = (bf16[512,256]{1,0:T(8,128)(2,1)S(1)}, bf16[512,256]{1,0:T(8,128)(2,1)S(1)}, u32[]{:S(2)}, u32[]{:S(2)}) collective-permute-start(bf16[512,256]{1,0:T(8,128)(2,1)S(1)} %get-tuple-element.33), channel_id=1, source_target_pairs={{0,6},{1,7},{8,14},{9,15},{64,70},{65,71},{72,78},{73,79},{16,22},... | collective-permute-start | bytes 786440 | tf_op jit(solution)/shard_map/ppermute | solution.py:39
  85.9 12.0 %collective-permute-start.16 = (bf16[512,256]{1,0:T(8,128)(2,1)S(1)}, bf16[512,256]{1,0:T(8,128)(2,1)S(1)}, u32[]{:S(2)}, u32[]{:S(2)}) collective-permute-start(bf16[512,256]{1,0:T(8,128)(2,1)S(1)} %get-tuple-element.31), channel_id=1, source_target_pairs={{0,6},{1,7},{8,14},{9,15},{64,70},{65,71},{72,78},{73,79},{16,22},... | collective-permute-start | bytes 786440 | tf_op jit(solution)/shard_map/ppermute | solution.py:39
  86.1 11.9 %collective-permute-start.24 = (bf16[512,256]{1,0:T(8,128)(2,1)S(1)}, bf16[512,256]{1,0:T(8,128)(2,1)S(1)}, u32[]{:S(2)}, u32[]{:S(2)}) collective-permute-start(bf16[512,256]{1,0:T(8,128)(2,1)S(1)} %get-tuple-element.30), channel_id=1, source_target_pairs={{0,2},{1,3},{8,10},{9,11},{64,66},{65,67},{72,74},{73,75},{16,18},... | collective-permute-start | bytes 786440 | tf_op jit(solution)/shard_map/ppermute | solution.py:39
  97.9 7.6 %collective-permute-start.28 = (bf16[512,256]{1,0:T(8,128)(2,1)S(1)}, bf16[512,256]{1,0:T(8,128)(2,1)S(1)}, u32[]{:S(2)}, u32[]{:S(2)}) collective-permute-start(bf16[512,256]{1,0:T(8,128)(2,1)S(1)} %get-tuple-element.27), channel_id=1, source_target_pairs={{0,6},{1,7},{8,14},{9,15},{64,70},{65,71},{72,78},{73,79},{16,22},... | collective-permute-start | bytes 786440 | tf_op jit(solution)/shard_map/ppermute | solution.py:39
  98.0 14.1 %collective-permute-start.13 = (bf16[512,256]{1,0:T(8,128)(2,1)S(1)}, bf16[512,256]{1,0:T(8,128)(2,1)S(1)}, u32[]{:S(2)}, u32[]{:S(2)}) collective-permute-start(bf16[512,256]{1,0:T(8,128)(2,1)S(1)} %fusion.3), channel_id=1, source_target_pairs={{0,2},{1,3},{8,10},{9,11},{64,66},{65,67},{72,74},{73,75},{16,18},... | collective-permute-start | bytes 786440 | tf_op jit(solution)/shard_map/ppermute | solution.py:39
  105.5 10.4 %collective-permute-start.17 = (bf16[512,256]{1,0:T(8,128)(2,1)S(1)}, bf16[512,256]{1,0:T(8,128)(2,1)S(1)}, u32[]{:S(2)}, u32[]{:S(2)}) collective-permute-start(bf16[512,256]{1,0:T(8,128)(2,1)S(1)} %fusion.2), channel_id=1, source_target_pairs={{0,6},{1,7},{8,14},{9,15},{64,70},{65,71},{72,78},{73,79},{16,22},... | collective-permute-start | bytes 786440 | tf_op jit(solution)/shard_map/ppermute | solution.py:39
  105.6 10.5 %collective-permute-start.26 = (bf16[512,256]{1,0:T(8,128)(2,1)S(1)}, bf16[512,256]{1,0:T(8,128)(2,1)S(1)}, u32[]{:S(2)}, u32[]{:S(2)}) collective-permute-start(bf16[512,256]{1,0:T(8,128)(2,1)S(1)} %get-tuple-element.28), channel_id=1, source_target_pairs={{0,2},{1,3},{8,10},{9,11},{64,66},{65,67},{72,74},{73,75},{16,18},... | collective-permute-start | bytes 786440 | tf_op jit(solution)/shard_map/ppermute | solution.py:39
  108.9 12.2 %collective-permute-start.27 = (bf16[512,256]{1,0:T(8,128)(2,1)S(1)}, bf16[512,256]{1,0:T(8,128)(2,1)S(1)}, u32[]{:S(2)}, u32[]{:S(2)}) collective-permute-start(bf16[512,256]{1,0:T(8,128)(2,1)S(1)} %get-tuple-element.29), channel_id=1, source_target_pairs={{0,6},{1,7},{8,14},{9,15},{64,70},{65,71},{72,78},{73,79},{16,22},... | collective-permute-start | bytes 786440 | tf_op jit(solution)/shard_map/ppermute | solution.py:39
  108.9 12.2 %collective-permute-start.25 = (bf16[512,256]{1,0:T(8,128)(2,1)S(1)}, bf16[512,256]{1,0:T(8,128)(2,1)S(1)}, u32[]{:S(2)}, u32[]{:S(2)}) collective-permute-start(bf16[512,256]{1,0:T(8,128)(2,1)S(1)} %fusion.1), channel_id=1, source_target_pairs={{0,2},{1,3},{8,10},{9,11},{64,66},{65,67},{72,74},{73,75},{16,18},... | collective-permute-start | bytes 786440 | tf_op jit(solution)/shard_map/ppermute | solution.py:39
  112.1 11.7 %collective-permute-start.29 = (bf16[512,256]{1,0:T(8,128)(2,1)S(1)}, bf16[512,256]{1,0:T(8,128)(2,1)S(1)}, u32[]{:S(2)}, u32[]{:S(2)}) collective-permute-start(bf16[512,256]{1,0:T(8,128)(2,1)S(1)} %fusion), channel_id=1, source_target_pairs={{0,6},{1,7},{8,14},{9,15},{64,70},{65,71},{72,78},{73,79},{16,22},... | collective-permute-start | bytes 786440 | tf_op jit(solution)/shard_map/ppermute | solution.py:39
  115.9 14.1 %collective-permute-start.35 = (f32[32,1024]{1,0:T(8,128)S(1)}, f32[32,1024]{1,0:T(8,128)S(1)}, u32[]{:S(2)}, u32[]{:S(2)}) collective-permute-start(f32[32,1024]{1,0:T(8,128)S(1)} %add.136.low_ref), channel_id=1, source_target_pairs={{0,6},{1,7},{8,14},{9,15},{64,70},{65,71},{72,78},{73,79},{16,22},... | collective-permute-start | bytes 393224 | tf_op jit(solution)/shard_map/ppermute | solution.py:39
  116.1 31.5 %collective-permute-start.18 = (bf16[1024,256]{1,0:T(8,128)(2,1)S(1)}, bf16[1024,256]{1,0:T(8,128)(2,1)S(1)}, u32[]{:S(2)}, u32[]{:S(2)}) collective-permute-start(bf16[1024,256]{1,0:T(8,128)(2,1)S(1)} %shard_map.88.own_ref), channel_id=1, source_target_pairs={{8,0},{9,1},{64,72},{65,73},{24,16},{25,17},{80,88},{81,89},{40,32... | collective-permute-start | bytes 1572872 | tf_op jit(solution)/shard_map/ppermute | solution.py:39
  124.1 23.6 %collective-permute-start.30 = (bf16[1024,256]{1,0:T(8,128)(2,1)S(1)}, bf16[1024,256]{1,0:T(8,128)(2,1)S(1)}, u32[]{:S(2)}, u32[]{:S(2)}) collective-permute-start(bf16[1024,256]{1,0:T(8,128)(2,1)S(1)} %shard_map.91), channel_id=1, source_target_pairs={{0,64},{1,65},{72,8},{73,9},{16,80},{17,81},{88,24},{89,25},{32,96... | collective-permute-start | bytes 1572872 | tf_op jit(solution)/shard_map/ppermute | solution.py:39
  129.2 18.4 %collective-permute-start.31 = (bf16[1024,256]{1,0:T(8,128)(2,1)S(1)}, bf16[1024,256]{1,0:T(8,128)(2,1)S(1)}, u32[]{:S(2)}, u32[]{:S(2)}) collective-permute-start(bf16[1024,256]{1,0:T(8,128)(2,1)S(1)} %shard_map.91), channel_id=1, source_target_pairs={{8,64},{9,65},{64,8},{65,9},{24,80},{25,81},{80,24},{81,25},{40,96... | collective-permute-start | bytes 1572872 | tf_op jit(solution)/shard_map/ppermute | solution.py:39
  130.4 4.4 %collective-permute-start.36 = (f32[16,1152]{1,0:T(8,128)S(1)}, f32[16,1152]{1,0:T(8,128)S(1)}, u32[]{:S(2)}, u32[]{:S(2)}) collective-permute-start(f32[16,1152]{1,0:T(8,128)S(1)} %get-tuple-element.26), channel_id=1, source_target_pairs={{0,16},{1,17},{8,24},{9,25},{64,80},{65,81},{72,88},{73,89},{16,0}... | collective-permute-start | bytes 221192 | tf_op jit(solution)/shard_map/ppermute | solution.py:39
  134.8 5.6 %collective-permute-start.37 = (f32[16,1152]{1,0:T(8,128)S(1)}, f32[16,1152]{1,0:T(8,128)S(1)}, u32[]{:S(2)}, u32[]{:S(2)}) collective-permute-start(f32[16,1152]{1,0:T(8,128)S(1)} %add.137), channel_id=1, source_target_pairs={{0,48},{1,49},{8,56},{9,57},{64,112},{65,113},{72,120},{73,121},{1... | collective-permute-start | bytes 221192 | tf_op jit(solution)/shard_map/ppermute | solution.py:39
  140.5 5.9 %collective-permute-start.38 = (f32[16,1152]{1,0:T(8,128)S(1)}, f32[16,1152]{1,0:T(8,128)S(1)}, u32[]{:S(2)}, u32[]{:S(2)}) collective-permute-start(f32[16,1152]{1,0:T(8,128)S(1)} %add.138), channel_id=1, source_target_pairs={{0,64},{1,65},{8,72},{9,73},{64,0},{65,1},{72,8},{73,9},{16,80},{1... | collective-permute-start | bytes 221192 | tf_op jit(solution)/shard_map/ppermute | solution.py:39

commit v2 on v1

--- a/solution.py
+++ b/solution.py
@@ -100,15 +100,17 @@
 
 
 def product_kernel(chunks, keep, *refs):
-    a_refs, b_refs, pieces = refs[:chunks], refs[chunks : 2 * chunks], refs[2 * chunks :]
+    a_refs, b_refs, pieces = refs[: chunks[0]], refs[chunks[0] : sum(chunks)], refs[sum(chunks) :]
     out_refs = refs[-2:]
     _, y, _, x, k = place()
     core = k if keep else 1 - k
     block = out_refs[0].shape[1]
-    each = a_refs[0].shape[0] // block
+
+    def half(of, i):
+        return of[i][...] if len(of) == 2 else of[0][i * block : (i + 1) * block, :]
+
     for i in range(2):
-        at = pl.ds((i % each) * block, block)
-        left = jnp.concatenate([a_refs[i // each][at, :], b_refs[i // each][at, :]], axis=1)
+        left = jnp.concatenate([half(a_refs, i), half(b_refs, i)], axis=1)
         for r in range(4):
             if r == 2:
                 kept = jnp.concatenate([pieces[4][core], pieces[5][core]], axis=0)
@@ -128,7 +130,7 @@
     args = [*a, *b, *pieces]
     vmem = pl.BlockSpec(memory_space=pltpu.VMEM)
     return pl.pallas_call(
-        functools.partial(product_kernel, len(a), keep),
+        functools.partial(product_kernel, (len(a), len(b)), keep),
         in_specs=[vmem] * len(args),
         out_specs=[vmem] * 2,
         out_shape=[jax.ShapeDtypeStruct((4, rows // 2, cols), F32 if keep else BF16)] * 2,
@@ -167,42 +169,44 @@
     )(low, more, x, grad_y)
 
 
-def finish_kernel(own_ref, own_moved_ref, far_moved_ref, near_moved_ref, low_ref, down_ref, out_ref):
+def finish_kernel(
+    own_ref, own_moved_ref, far_a, far_b, near_a, near_b, low_ref, down_ref, out_ref
+):
     zh, _, zl, _, _ = place()
     stays = zh == zl
-    first = jnp.where(stays, own_ref[...], far_moved_ref[...])
-    second = jnp.where(stays, own_moved_ref[...], near_moved_ref[...])
-    adapter = 2.0 * lax.dot_general(
-        low_ref[RANK:], down_ref[...], (((0,), (0,)), ((), ())), preferred_element_type=F32
-    )
+    cut = far_a.shape[0]
     cols = own_ref.shape[1]
-    left = jnp.where(zl == 0, first, second)
-    right = jnp.where(zl == 0, second, first)
-    out_ref[:, :cols] = (left.astype(F32) + adapter[:, :cols]).astype(BF16)
-    out_ref[:, cols:] = (right.astype(F32) + adapter[:, cols:]).astype(BF16)
-
-
-def finish(own, own_moved, far_moved, near_moved, low, down_t):
+    block = 128
+    for start in range(0, own_ref.shape[0], block):
+        at = slice(start, start + block)
+        far, near = (far_a[at, :], near_a[at, :]) if start < cut else (
+            far_b[start - cut : start - cut + block, :],
+            near_b[start - cut : start - cut + block, :],
+        )
+        first = jnp.where(stays, own_ref[at, :], far)
+        second = jnp.where(stays, own_moved_ref[at, :], near)
+        adapter = 2.0 * lax.dot_general(
+            low_ref[RANK:, at], down_ref[...], (((0,), (0,)), ((), ())), preferred_element_type=F32
+        )
+        left = jnp.where(zl == 0, first, second)
+        right = jnp.where(zl == 0, second, first)
+        out_ref[at, :cols] = (left.astype(F32) + adapter[:, :cols]).astype(BF16)
+        out_ref[at, cols:] = (right.astype(F32) + adapter[:, cols:]).astype(BF16)
+
+
+def finish(own, own_moved, far, near, low, down_t):
     rows, cols = own.shape
-    block = 256
-    half = pl.BlockSpec((block, cols), lambda i: (i, 0))
+    vmem = pl.BlockSpec(memory_space=pltpu.VMEM)
     return pl.pallas_call(
         finish_kernel,
-        grid=(rows // block,),
-        in_specs=[half] * 4
-        + [
-            pl.BlockSpec((2 * RANK, block), lambda i: (0, i)),
-            pl.BlockSpec(down_t.shape, lambda i: (0, 0)),
-        ],
-        out_specs=pl.BlockSpec((block, 2 * cols), lambda i: (i, 0)),
+        in_specs=[vmem] * 8,
+        out_specs=vmem,
         out_shape=jax.ShapeDtypeStruct((rows, 2 * cols), BF16),
-        compiler_params=pltpu.CompilerParams(
-            dimension_semantics=("arbitrary",), vmem_limit_bytes=8 << 20
-        ),
+        compiler_params=pltpu.CompilerParams(vmem_limit_bytes=12 << 20),
         cost_estimate=pl.CostEstimate(
             flops=64 * rows * cols, bytes_accessed=12 * rows * cols, transcendentals=0
         ),
-    )(own, own_moved, far_moved, near_moved, low, down_t)
+    )(own, own_moved, *far, *near, low, down_t)
 
 
 def add_up_kernel(*refs):
@@ -266,11 +270,12 @@
     cosine, sine, down_t = jnp.cos(angle), jnp.sin(angle), down.T
     grad_y, low = rotate(gradient, cosine, sine, swap, normed_input, down_t, up)
 
-    near = send(grad_y, zx=1)
+    mid = rows // 2
+    near_low = send(grad_y[mid:], zx=1)
+    near_top = send(grad_y[:mid], zx=1)
     cross = send(grad_y, zx=3)
-    mid = rows // 2
     far_top = send(cross[:mid], zx=1)
-    far_low = send(near[mid:], zx=3)
+    far_low = send(near_low, zx=3)
 
     low = low + send(low, zx=1)
     low = low + send(low, dk=1)
@@ -284,9 +289,7 @@
     grad_a, grad_b = parts[:, : down.shape[0]].T, parts[:, down.shape[0] :]
 
     sums = []
-    for a, b in (([grad_y], [near]), ([far_top, far_low], [cross])):
-        if len(a) != len(b):
-            b = [b[0][:mid], b[0][mid:]]
+    for a, b in (([grad_y], [near_top, near_low]), ([far_top, far_low], [cross])):
         partial = product(a, b, pieces, False)
         arrived = [send(p, dk=1) for p in partial]
         total = product(a, b, pieces, True)
@@ -294,9 +297,13 @@
     own, opposite = sums
 
     own_moved = send(own, zmap={1: 0, 2: 3})
-    far_moved = send(opposite, zmap={0: 2, 3: 1})
-    near_moved = send(opposite, zmap={1: 2, 2: 1})
-    grad_x = finish(own, own_moved, far_moved, near_moved, low, down_t)
+    cut = 640
+    top, low_rows = opposite[:cut], opposite[cut:]
+    near_a = send(top, zx=3)
+    near_b = send(low_rows, zmap={1: 2, 2: 1})
+    far_a = send(near_a, zmap={3: 2, 0: 1})
+    far_b = send(low_rows, zmap={0: 2, 3: 1})
+    grad_x = finish(own, own_moved, (far_a, far_b), (near_a, near_b), low, down_t)
     return grad_x, grad_a, grad_b
 
 

time: 150 us -> 177 us (1.18)
  the two profiles are of different devices: /device:TPU:6 before, /device:TPU:32 now
where the time goes in v2:
time: 177 us; the launch traced here: 176 us
  waiting for transfers between devices  90.8 us (51%)
  starting transfers between devices  57.6 us (33%)
  Pallas kernels  16.5 us (9%)
  local copies, waits for them, and re-layouts  6.95 us (4%)
  other arithmetic  3.49 us (2%)
    ppermute x42, waiting for transfers between devices, send(): return lax.ppermute(value, AXES, pairs)  90.8 us
    ppermute x42, starting transfers between devices, send(): return lax.ppermute(value, AXES, pairs)  57.6 us
    pallas_call x4, Pallas kernels, product(): pl.pallas_call(functools.partial(product_kernel, (len(a), len(b)), keep),...  12.1 us
    unnamed x12, local copies, waits for them, and re-layouts  3.99 us
  transfers between devices with their start and end apart: 42, of which 18 were waited for; matrix products, arithmetic and copies ran while one was open for 2% of the time, Pallas kernels for 7%

profile of v2, /device:TPU:32, one launch (start us, length us, event | category | flops | bytes accessed | tf_op | source)
XLA Modules:
  0.0 176.3 jit_solution(3964328500601284903)
XLA Ops:
  1.4 1.9 %multiply_sine_fusion = (f32[1024,128]{1,0:T(8,128)S(1)}, f32[1024,128]{1,0:T(8,128)S(1)}) fusion(f32[128]{0:T(128)S(1)} %fusion.14, f32[1024]{0:T(1024)S(1)} %convert_element_type.133), kind=kLoop, calls=%fused_computation | loop fusion | flops 131072 | bytes 1053184 | tf_op jit(solution)/shard_map/sin | solution.py:270
  3.3 1.2 copy-done
  4.5 1.3 copy-done.2
  7.3 2.1 %shard_map.85 = (bf16[1024,640]{1,0:T(8,128)(2,1)S(1)}, f32[32,1024]{1,0:T(8,128)S(1)}) custom-call(bf16[1024,640]{1,0:T(8,128)(2,1)S(1)} %copy-done.2, f32[1024,128]{1,0:T(8,128)S(1)} %get-tuple-element.40.cos_ref, f32[1024,128]{1,0:T(8,128)S(1)} %get-tuple-element.39.sin_ref, bf16[128,128]{1,0:T(8,128)(2,1)S(1)} %select_convert_fusion.swap_ref, ...), custom_call_target="tpu_custom_call" | custom-call | flops 209715200 | bytes 5242880 | tf_op jit(solution)/shard_map/pallas_call | solution.py:76
  9.3 1.9 %collective-permute-start.20 = (bf16[1024,640]{1,0:T(8,128)(2,1)S(1)}, bf16[1024,640]{1,0:T(8,128)(2,1)S(1)}, u32[]{:S(2)}, u32[]{:S(2)}) collective-permute-start(bf16[1024,640]{1,0:T(8,128)(2,1)S(1)} %get-tuple-element.15.refs_0_.y_ref), channel_id=1, source_target_pairs={{0,72},{1,73},{8,64},{9,65},{64,8},{65,9},{72,0},{73,1},{16,88},{1... | collective-permute-start | bytes 3932168 | tf_op jit(solution)/shard_map/ppermute | solution.py:39
  11.3 1.4 dynamic-slice_bitcast_fusion
  12.7 2.3 %collective-permute-start.2 = (bf16[2,256,640]{2,1,0:T(8,128)(2,1)S(1)}, bf16[2,256,640]{2,1,0:T(8,128)(2,1)S(1)}, u32[]{:S(2)}, u32[]{:S(2)}) collective-permute-start(bf16[2,256,640]{2,1,0:T(8,128)(2,1)S(1)} %get-tuple-element.35), channel_id=1, source_target_pairs={{0,8},{1,9},{8,0},{9,1},{64,72},{65,73},{72,64},{73,65},{16,24},{1... | collective-permute-start | bytes 1966088 | tf_op jit(solution)/shard_map/ppermute | solution.py:39
  15.2 1.6 collective-permute-start.5
  16.8 1.7 collective-permute-start.3
  18.5 12.1 %collective-permute-done.2.refs_4_ = bf16[2,256,640]{2,1,0:T(8,128)(2,1)S(1)} collective-permute-done((bf16[2,256,640]{2,1,0:T(8,128)(2,1)S(1)}, bf16[2,256,640]{2,1,0:T(8,128)(2,1)S(1)}, u32[]{:S(2)}, u32[]{:S(2)}) %collective-permute-start.2) | collective-permute-done | bytes 655392 | tf_op jit(solution)/shard_map/ppermute | solution.py:39
  30.6 1.6 collective-permute-start.8
  32.1 11.3 %collective-permute-done.1.refs_2_ = bf16[512,640]{1,0:T(8,128)(2,1)S(1)} collective-permute-done((bf16[512,640]{1,0:T(8,128)(2,1)S(1)}, bf16[512,640]{1,0:T(8,128)(2,1)S(1)}, u32[]{:S(2)}, u32[]{:S(2)}) %collective-permute-start.1) | collective-permute-done | bytes 655392 | tf_op jit(solution)/shard_map/ppermute | solution.py:39
  43.5 3.0 %collective-permute-start.4 = (bf16[2,256,640]{2,1,0:T(8,128)(2,1)S(1)}, bf16[2,256,640]{2,1,0:T(8,128)(2,1)S(1)}, u32[]{:S(2)}, u32[]{:S(2)}) collective-permute-start(bf16[2,256,640]{2,1,0:T(8,128)(2,1)S(1)} %collective-permute-done.2.refs_4_), channel_id=1, source_target_pairs={{0,48},{1,49},{8,56},{9,57},{64,112},{65,113},{72,120},{73,121},{1... | collective-permute-start | bytes 1966088 | tf_op jit(solution)/shard_map/ppermute | solution.py:39
  46.5 1.7 collective-permute-start
  49.3 10.3 %collective-permute-done.4.refs_6_ = bf16[2,256,640]{2,1,0:T(8,128)(2,1)S(1)} collective-permute-done((bf16[2,256,640]{2,1,0:T(8,128)(2,1)S(1)}, bf16[2,256,640]{2,1,0:T(8,128)(2,1)S(1)}, u32[]{:S(2)}, u32[]{:S(2)}) %collective-permute-start.4) | collective-permute-done | bytes 655392 | tf_op jit(solution)/shard_map/ppermute | solution.py:39
  59.6 3.7 %collective-permute-start.7 = (bf16[2,128,640]{2,1,0:T(8,128)(2,1)S(1)}, bf16[2,128,640]{2,1,0:T(8,128)(2,1)S(1)}, u32[]{:S(2)}, u32[]{:S(2)}) collective-permute-start(bf16[2,128,640]{2,1,0:T(8,128)(2,1)S(1)} %slice.141), channel_id=1, source_target_pairs={{0,48},{1,49},{8,56},{9,57},{64,112},{65,113},{72,120},{73,121},{1... | collective-permute-start | bytes 983048 | tf_op jit(solution)/shard_map/ppermute | solution.py:39
  64.1 3.2 %collective-permute-start.10 = (bf16[2,128,640]{2,1,0:T(8,128)(2,1)S(1)}, bf16[2,128,640]{2,1,0:T(8,128)(2,1)S(1)}, u32[]{:S(2)}, u32[]{:S(2)}) collective-permute-start(bf16[2,128,640]{2,1,0:T(8,128)(2,1)S(1)} %slice.143), channel_id=1, source_target_pairs={{0,48},{1,49},{8,56},{9,57},{64,112},{65,113},{72,120},{73,121},{1... | collective-permute-start | bytes 983048 | tf_op jit(solution)/shard_map/ppermute | solution.py:39
  67.3 4.1 %collective-permute-done.7.refs_8_ = bf16[2,128,640]{2,1,0:T(8,128)(2,1)S(1)} collective-permute-done((bf16[2,128,640]{2,1,0:T(8,128)(2,1)S(1)}, bf16[2,128,640]{2,1,0:T(8,128)(2,1)S(1)}, u32[]{:S(2)}, u32[]{:S(2)}) %collective-permute-start.7) | collective-permute-done | bytes 327712 | tf_op jit(solution)/shard_map/ppermute | solution.py:39
  72.4 3.2 %collective-permute-done.10.refs_10_ = bf16[2,128,640]{2,1,0:T(8,128)(2,1)S(1)} collective-permute-done((bf16[2,128,640]{2,1,0:T(8,128)(2,1)S(1)}, bf16[2,128,640]{2,1,0:T(8,128)(2,1)S(1)}, u32[]{:S(2)}, u32[]{:S(2)}) %collective-permute-start.10) | collective-permute-done | bytes 327712 | tf_op jit(solution)/shard_map/ppermute | solution.py:39
  75.6 3.0 %shard_map.87 = (bf16[4,512,256]{2,1,0:T(8,128)(2,1)S(1)}, bf16[4,512,256]{2,1,0:T(8,128)(2,1)S(1)}) custom-call(bf16[1024,640]{1,0:T(8,128)(2,1)S(1)} %get-tuple-element.15.refs_0_.y_ref, bf16[512,640]{1,0:T(8,128)(2,1)S(1)} %collective-permute-done.refs_1_, bf16[512,640]{1,0:T(8,128)(2,1)S(1)} %collective-permute-done.1.refs_2_, ...), custom_call_target="tpu_custom_call" | custom-call | flops 2684354560 | bytes 7340032 | tf_op jit(solution)/shard_map/pallas_call | solution.py:132
  78.7 3.0 %shard_map.90 = (bf16[4,512,256]{2,1,0:T(8,128)(2,1)S(1)}, bf16[4,512,256]{2,1,0:T(8,128)(2,1)S(1)}) custom-call(bf16[512,640]{1,0:T(8,128)(2,1)S(1)} %collective-permute-done.21.refs_0_, bf16[512,640]{1,0:T(8,128)(2,1)S(1)} %collective-permute-done.22.refs_1_, bf16[1024,640]{1,0:T(8,128)(2,1)S(1)} %collective-permute-done.20.refs_2_, ...), custom_call_target="tpu_custom_call" | custom-call | flops 2684354560 | bytes 7340032 | tf_op jit(solution)/shard_map/pallas_call | solution.py:132
  82.3 1.2 collective-permute-start.35
  83.4 4.3 %collective-permute-done.35 = f32[32,1024]{1,0:T(8,128)S(1)} collective-permute-done((f32[32,1024]{1,0:T(8,128)S(1)}, f32[32,1024]{1,0:T(8,128)S(1)}, u32[]{:S(2)}, u32[]{:S(2)}) %collective-permute-start.35) | collective-permute-done | bytes 131104 | tf_op jit(solution)/shard_map/ppermute | solution.py:39
  88.4 3.0 %shard_map.86 = (f32[4,512,256]{2,1,0:T(8,128)S(1)}, f32[4,512,256]{2,1,0:T(8,128)S(1)}) custom-call(bf16[1024,640]{1,0:T(8,128)(2,1)S(1)} %get-tuple-element.15.refs_0_.y_ref, bf16[512,640]{1,0:T(8,128)(2,1)S(1)} %collective-permute-done.refs_1_, bf16[512,640]{1,0:T(8,128)(2,1)S(1)} %collective-permute-done.1.refs_2_, ...), custom_call_target="tpu_custom_call" | custom-call | flops 2684354560 | bytes 7340032 | tf_op jit(solution)/shard_map/pallas_call | solution.py:132
  91.4 3.1 %shard_map.89 = (f32[4,512,256]{2,1,0:T(8,128)S(1)}, f32[4,512,256]{2,1,0:T(8,128)S(1)}) custom-call(bf16[512,640]{1,0:T(8,128)(2,1)S(1)} %collective-permute-done.21.refs_0_, bf16[512,640]{1,0:T(8,128)(2,1)S(1)} %collective-permute-done.22.refs_1_, bf16[1024,640]{1,0:T(8,128)(2,1)S(1)} %collective-permute-done.20.refs_2_, ...), custom_call_target="tpu_custom_call" | custom-call | flops 2684354560 | bytes 7340032 | tf_op jit(solution)/shard_map/pallas_call | solution.py:132
  94.6 1.5 collective-permute-start.13
  96.3 1.6 collective-permute-start.25
  98.0 1.8 %collective-permute-start.29 = (bf16[512,256]{1,0:T(8,128)(2,1)S(1)}, bf16[512,256]{1,0:T(8,128)(2,1)S(1)}, u32[]{:S(2)}, u32[]{:S(2)}) collective-permute-start(bf16[512,256]{1,0:T(8,128)(2,1)S(1)} %get-tuple-element.27), channel_id=1, source_target_pairs={{0,6},{1,7},{8,14},{9,15},{64,70},{65,71},{72,78},{73,79},{16,22},... | collective-permute-start | bytes 786440 | tf_op jit(solution)/shard_map/ppermute | solution.py:39
  100.6 9.3 %collective-permute-done.25 = bf16[512,256]{1,0:T(8,128)(2,1)S(1)} collective-permute-done((bf16[512,256]{1,0:T(8,128)(2,1)S(1)}, bf16[512,256]{1,0:T(8,128)(2,1)S(1)}, u32[]{:S(2)}, u32[]{:S(2)}) %collective-permute-start.25) | collective-permute-done | bytes 262176 | tf_op jit(solution)/shard_map/ppermute | solution.py:39
  110.2 3.1 %collective-permute-start.28 = (bf16[512,256]{1,0:T(8,128)(2,1)S(1)}, bf16[512,256]{1,0:T(8,128)(2,1)S(1)}, u32[]{:S(2)}, u32[]{:S(2)}) collective-permute-start(bf16[512,256]{1,0:T(8,128)(2,1)S(1)} %get-tuple-element.29), channel_id=1, source_target_pairs={{0,6},{1,7},{8,14},{9,15},{64,70},{65,71},{72,78},{73,79},{16,22},... | collective-permute-start | bytes 786440 | tf_op jit(solution)/shard_map/ppermute | solution.py:39
  113.4 3.2 %collective-permute-start.30 = (bf16[512,256]{1,0:T(8,128)(2,1)S(1)}, bf16[512,256]{1,0:T(8,128)(2,1)S(1)}, u32[]{:S(2)}, u32[]{:S(2)}) collective-permute-start(bf16[512,256]{1,0:T(8,128)(2,1)S(1)} %fusion), channel_id=1, source_target_pairs={{0,6},{1,7},{8,14},{9,15},{64,70},{65,71},{72,78},{73,79},{16,22},... | collective-permute-start | bytes 786440 | tf_op jit(solution)/shard_map/ppermute | solution.py:39
  116.9 3.3 %collective-permute-done.27.refs_5_ = bf16[512,256]{1,0:T(8,128)(2,1)S(1)} collective-permute-done((bf16[512,256]{1,0:T(8,128)(2,1)S(1)}, bf16[512,256]{1,0:T(8,128)(2,1)S(1)}, u32[]{:S(2)}, u32[]{:S(2)}) %collective-permute-start.27) | collective-permute-done | bytes 262176 | tf_op jit(solution)/shard_map/ppermute | solution.py:39
  120.6 1.7 collective-permute-start.14
  122.3 3.6 %collective-permute-done.26.refs_4_ = bf16[512,256]{1,0:T(8,128)(2,1)S(1)} collective-permute-done((bf16[512,256]{1,0:T(8,128)(2,1)S(1)}, bf16[512,256]{1,0:T(8,128)(2,1)S(1)}, u32[]{:S(2)}, u32[]{:S(2)}) %collective-permute-start.26) | collective-permute-done | bytes 262176 | tf_op jit(solution)/shard_map/ppermute | solution.py:39
  126.2 1.8 %collective-permute-start.37 = (f32[32,1024]{1,0:T(8,128)S(1)}, f32[32,1024]{1,0:T(8,128)S(1)}, u32[]{:S(2)}, u32[]{:S(2)}) collective-permute-start(f32[32,1024]{1,0:T(8,128)S(1)} %add.135), channel_id=1, source_target_pairs={{0,2},{1,3},{8,10},{9,11},{64,66},{65,67},{72,74},{73,75},{16,18},... | collective-permute-start | bytes 393224 | tf_op jit(solution)/shard_map/ppermute | solution.py:39
  128.3 8.9 %collective-permute-done.37 = f32[32,1024]{1,0:T(8,128)S(1)} collective-permute-done((f32[32,1024]{1,0:T(8,128)S(1)}, f32[32,1024]{1,0:T(8,128)S(1)}, u32[]{:S(2)}, u32[]{:S(2)}) %collective-permute-start.37) | collective-permute-done | bytes 131104 | tf_op jit(solution)/shard_map/ppermute | solution.py:39
  137.2 1.5 collective-permute-start.38
  138.9 4.0 %collective-permute-start.19 = (bf16[1024,256]{1,0:T(8,128)(2,1)S(1)}, bf16[1024,256]{1,0:T(8,128)(2,1)S(1)}, u32[]{:S(2)}, u32[]{:S(2)}) collective-permute-start(bf16[1024,256]{1,0:T(8,128)(2,1)S(1)} %shard_map.88.own_ref), channel_id=1, source_target_pairs={{8,0},{9,1},{64,72},{65,73},{24,16},{25,17},{80,88},{81,89},{40,32... | collective-permute-start | bytes 1572872 | tf_op jit(solution)/shard_map/ppermute | solution.py:39
  143.9 4.3 %collective-permute-done.39 = f32[16,1152]{1,0:T(8,128)S(1)} collective-permute-done((f32[16,1152]{1,0:T(8,128)S(1)}, f32[16,1152]{1,0:T(8,128)S(1)}, u32[]{:S(2)}, u32[]{:S(2)}) %collective-permute-start.39) | collective-permute-done | bytes 73760 | tf_op jit(solution)/shard_map/ppermute | solution.py:39
  148.3 3.8 %collective-permute-start.40 = (f32[16,1152]{1,0:T(8,128)S(1)}, f32[16,1152]{1,0:T(8,128)S(1)}, u32[]{:S(2)}, u32[]{:S(2)}) collective-permute-start(f32[16,1152]{1,0:T(8,128)S(1)} %add.137), channel_id=1, source_target_pairs={{0,48},{1,49},{8,56},{9,57},{64,112},{65,113},{72,120},{73,121},{1... | collective-permute-start | bytes 221192 | tf_op jit(solution)/shard_map/ppermute | solution.py:39
  152.1 1.3 collective-permute-start.32
  154.4 3.3 %collective-permute-start.41 = (f32[16,1152]{1,0:T(8,128)S(1)}, f32[16,1152]{1,0:T(8,128)S(1)}, u32[]{:S(2)}, u32[]{:S(2)}) collective-permute-start(f32[16,1152]{1,0:T(8,128)S(1)} %add.138), channel_id=1, source_target_pairs={{0,64},{1,65},{8,72},{9,73},{64,0},{65,1},{72,8},{73,9},{16,80},{1... | collective-permute-start | bytes 221192 | tf_op jit(solution)/shard_map/ppermute | solution.py:39
  157.7 5.6 %collective-permute-done.41 = f32[16,1152]{1,0:T(8,128)S(1)} collective-permute-done((f32[16,1152]{1,0:T(8,128)S(1)}, f32[16,1152]{1,0:T(8,128)S(1)}, u32[]{:S(2)}, u32[]{:S(2)}) %collective-permute-start.41) | collective-permute-done | bytes 73760 | tf_op jit(solution)/shard_map/ppermute | solution.py:39
  163.9 1.3 collective-permute-start.33
  165.2 1.9 %collective-permute-start.34 = (bf16[384,256]{1,0:T(8,128)(2,1)S(1)}, bf16[384,256]{1,0:T(8,128)(2,1)S(1)}, u32[]{:S(2)}, u32[]{:S(2)}) collective-permute-start(bf16[384,256]{1,0:T(8,128)(2,1)S(1)} %slice.158), channel_id=1, source_target_pairs={{8,64},{9,65},{64,8},{65,9},{24,80},{25,81},{80,24},{81,25},{40,96... | collective-permute-start | bytes 589832 | tf_op jit(solution)/shard_map/ppermute | solution.py:39
  167.8 5.3 %collective-permute-done.33.far_b = bf16[384,256]{1,0:T(8,128)(2,1)S(1)} collective-permute-done((bf16[384,256]{1,0:T(8,128)(2,1)S(1)}, bf16[384,256]{1,0:T(8,128)(2,1)S(1)}, u32[]{:S(2)}, u32[]{:S(2)}) %collective-permute-start.33) | collective-permute-done | bytes 196640 | tf_op jit(solution)/shard_map/ppermute | solution.py:39
  173.1 1.8 %collective-permute-done.34.near_b = bf16[384,256]{1,0:T(8,128)(2,1)S(1)} collective-permute-done((bf16[384,256]{1,0:T(8,128)(2,1)S(1)}, bf16[384,256]{1,0:T(8,128)(2,1)S(1)}, u32[]{:S(2)}, u32[]{:S(2)}) %collective-permute-start.34) | collective-permute-done | bytes 196640 | tf_op jit(solution)/shard_map/ppermute | solution.py:39
  174.9 1.4 shard_map.93
  (88 shorter events, 12.8 us)
Async XLA Ops:
  3.3 1.2 copy-start
  4.5 1.3 copy-start.2
  5.8 0.7 copy-start.3
  6.5 0.7 copy-start.5
  9.3 38.9 %collective-permute-start.20 = (bf16[1024,640]{1,0:T(8,128)(2,1)S(1)}, bf16[1024,640]{1,0:T(8,128)(2,1)S(1)}, u32[]{:S(2)}, u32[]{:S(2)}) collective-permute-start(bf16[1024,640]{1,0:T(8,128)(2,1)S(1)} %get-tuple-element.15.refs_0_.y_ref), channel_id=1, source_target_pairs={{0,72},{1,73},{8,64},{9,65},{64,8},{65,9},{72,0},{73,1},{16,88},{1... | collective-permute-start | bytes 3932168 | tf_op jit(solution)/shard_map/ppermute | solution.py:39
  12.7 17.9 %collective-permute-start.2 = (bf16[2,256,640]{2,1,0:T(8,128)(2,1)S(1)}, bf16[2,256,640]{2,1,0:T(8,128)(2,1)S(1)}, u32[]{:S(2)}, u32[]{:S(2)}) collective-permute-start(bf16[2,256,640]{2,1,0:T(8,128)(2,1)S(1)} %get-tuple-element.35), channel_id=1, source_target_pairs={{0,8},{1,9},{8,0},{9,1},{64,72},{65,73},{72,64},{73,65},{16,24},{1... | collective-permute-start | bytes 1966088 | tf_op jit(solution)/shard_map/ppermute | solution.py:39
  15.1 28.4 %collective-permute-start.1 = (bf16[512,640]{1,0:T(8,128)(2,1)S(1)}, bf16[512,640]{1,0:T(8,128)(2,1)S(1)}, u32[]{:S(2)}, u32[]{:S(2)}) collective-permute-start(bf16[512,640]{1,0:T(8,128)(2,1)S(1)} %get-tuple-element.37), channel_id=1, source_target_pairs={{0,8},{1,9},{8,0},{9,1},{64,72},{65,73},{72,64},{73,65},{16,24},{1... | collective-permute-start | bytes 1966088 | tf_op jit(solution)/shard_map/ppermute | solution.py:39
  15.2 31.3 %collective-permute-start.5 = (bf16[2,256,640]{2,1,0:T(8,128)(2,1)S(1)}, bf16[2,256,640]{2,1,0:T(8,128)(2,1)S(1)}, u32[]{:S(2)}, u32[]{:S(2)}) collective-permute-start(bf16[2,256,640]{2,1,0:T(8,128)(2,1)S(1)} %get-tuple-element.36.refs_3_), channel_id=1, source_target_pairs={{0,16},{1,17},{8,24},{9,25},{64,80},{65,81},{72,88},{73,89},{16,32... | collective-permute-start | bytes 1966088 | tf_op jit(solution)/shard_map/ppermute | solution.py:39
  16.8 31.6 %collective-permute-start.3 = (bf16[2,256,640]{2,1,0:T(8,128)(2,1)S(1)}, bf16[2,256,640]{2,1,0:T(8,128)(2,1)S(1)}, u32[]{:S(2)}, u32[]{:S(2)}) collective-permute-start(bf16[2,256,640]{2,1,0:T(8,128)(2,1)S(1)} %get-tuple-element.36.refs_3_), channel_id=1, source_target_pairs={{0,48},{1,49},{8,56},{9,57},{64,112},{65,113},{72,120},{73,121},{1... | collective-permute-start | bytes 1966088 | tf_op jit(solution)/shard_map/ppermute | solution.py:39
  30.6 18.0 %collective-permute-start.8 = (bf16[2,256,640]{2,1,0:T(8,128)(2,1)S(1)}, bf16[2,256,640]{2,1,0:T(8,128)(2,1)S(1)}, u32[]{:S(2)}, u32[]{:S(2)}) collective-permute-start(bf16[2,256,640]{2,1,0:T(8,128)(2,1)S(1)} %collective-permute-done.2.refs_4_), channel_id=1, source_target_pairs={{0,16},{1,17},{8,24},{9,25},{64,80},{65,81},{72,88},{73,89},{16,32... | collective-permute-start | bytes 1966088 | tf_op jit(solution)/shard_map/ppermute | solution.py:39
  43.5 16.2 %collective-permute-start.4 = (bf16[2,256,640]{2,1,0:T(8,128)(2,1)S(1)}, bf16[2,256,640]{2,1,0:T(8,128)(2,1)S(1)}, u32[]{:S(2)}, u32[]{:S(2)}) collective-permute-start(bf16[2,256,640]{2,1,0:T(8,128)(2,1)S(1)} %collective-permute-done.2.refs_4_), channel_id=1, source_target_pairs={{0,48},{1,49},{8,56},{9,57},{64,112},{65,113},{72,120},{73,121},{1... | collective-permute-start | bytes 1966088 | tf_op jit(solution)/shard_map/ppermute | solution.py:39
  46.5 17.6 %collective-permute-start = (bf16[512,640]{1,0:T(8,128)(2,1)S(1)}, bf16[512,640]{1,0:T(8,128)(2,1)S(1)}, u32[]{:S(2)}, u32[]{:S(2)}) collective-permute-start(bf16[512,640]{1,0:T(8,128)(2,1)S(1)} %get-tuple-element.38), channel_id=1, source_target_pairs={{0,8},{1,9},{8,0},{9,1},{64,72},{65,73},{72,64},{73,65},{16,24},{1... | collective-permute-start | bytes 1966088 | tf_op jit(solution)/shard_map/ppermute | solution.py:39
  48.3 15.8 %collective-permute-start.6 = (bf16[2,128,640]{2,1,0:T(8,128)(2,1)S(1)}, bf16[2,128,640]{2,1,0:T(8,128)(2,1)S(1)}, u32[]{:S(2)}, u32[]{:S(2)}) collective-permute-start(bf16[2,128,640]{2,1,0:T(8,128)(2,1)S(1)} %slice.140), channel_id=1, source_target_pairs={{0,16},{1,17},{8,24},{9,25},{64,80},{65,81},{72,88},{73,89},{16,32... | collective-permute-start | bytes 983048 | tf_op jit(solution)/shard_map/ppermute | solution.py:39
  48.4 30.2 %collective-permute-start.22 = (bf16[512,640]{1,0:T(8,128)(2,1)S(1)}, bf16[512,640]{1,0:T(8,128)(2,1)S(1)}, u32[]{:S(2)}, u32[]{:S(2)}) collective-permute-start(bf16[512,640]{1,0:T(8,128)(2,1)S(1)} %collective-permute-done.1.refs_2_), channel_id=1, source_target_pairs={{0,72},{1,73},{8,64},{9,65},{64,8},{65,9},{72,0},{73,1},{16,88},{1... | collective-permute-start | bytes 1966088 | tf_op jit(solution)/shard_map/ppermute | solution.py:39
  48.5 30.2 %collective-permute-start.21 = (bf16[512,640]{1,0:T(8,128)(2,1)S(1)}, bf16[512,640]{1,0:T(8,128)(2,1)S(1)}, u32[]{:S(2)}, u32[]{:S(2)}) collective-permute-start(bf16[512,640]{1,0:T(8,128)(2,1)S(1)} %slice.150), channel_id=1, source_target_pairs={{0,8},{1,9},{8,0},{9,1},{64,72},{65,73},{72,64},{73,65},{16,24},{1... | collective-permute-start | bytes 1966088 | tf_op jit(solution)/shard_map/ppermute | solution.py:39
  59.6 11.8 %collective-permute-start.7 = (bf16[2,128,640]{2,1,0:T(8,128)(2,1)S(1)}, bf16[2,128,640]{2,1,0:T(8,128)(2,1)S(1)}, u32[]{:S(2)}, u32[]{:S(2)}) collective-permute-start(bf16[2,128,640]{2,1,0:T(8,128)(2,1)S(1)} %slice.141), channel_id=1, source_target_pairs={{0,48},{1,49},{8,56},{9,57},{64,112},{65,113},{72,120},{73,121},{1... | collective-permute-start | bytes 983048 | tf_op jit(solution)/shard_map/ppermute | solution.py:39
  64.1 8.3 %collective-permute-start.9 = (bf16[2,128,640]{2,1,0:T(8,128)(2,1)S(1)}, bf16[2,128,640]{2,1,0:T(8,128)(2,1)S(1)}, u32[]{:S(2)}, u32[]{:S(2)}) collective-permute-start(bf16[2,128,640]{2,1,0:T(8,128)(2,1)S(1)} %slice.142), channel_id=1, source_target_pairs={{0,16},{1,17},{8,24},{9,25},{64,80},{65,81},{72,88},{73,89},{16,32... | collective-permute-start | bytes 983048 | tf_op jit(solution)/shard_map/ppermute | solution.py:39
  64.1 11.5 %collective-permute-start.10 = (bf16[2,128,640]{2,1,0:T(8,128)(2,1)S(1)}, bf16[2,128,640]{2,1,0:T(8,128)(2,1)S(1)}, u32[]{:S(2)}, u32[]{:S(2)}) collective-permute-start(bf16[2,128,640]{2,1,0:T(8,128)(2,1)S(1)} %slice.143), channel_id=1, source_target_pairs={{0,48},{1,49},{8,56},{9,57},{64,112},{65,113},{72,120},{73,121},{1... | collective-permute-start | bytes 983048 | tf_op jit(solution)/shard_map/ppermute | solution.py:39
  78.6 15.9 %collective-permute-start.11 = (bf16[4,512,256]{2,1,0:T(8,128)(2,1)S(1)}, bf16[4,512,256]{2,1,0:T(8,128)(2,1)S(1)}, u32[]{:S(2)}, u32[]{:S(2)}) collective-permute-start(bf16[4,512,256]{2,1,0:T(8,128)(2,1)S(1)} %get-tuple-element.18), channel_id=1, source_target_pairs={{0,1},{1,0},{8,9},{9,8},{64,65},{65,64},{72,73},{73,72},{16,17},{1... | collective-permute-start | bytes 3145736 | tf_op jit(solution)/shard_map/ppermute | solution.py:39
  81.7 14.5 %collective-permute-start.23 = (bf16[4,512,256]{2,1,0:T(8,128)(2,1)S(1)}, bf16[4,512,256]{2,1,0:T(8,128)(2,1)S(1)}, u32[]{:S(2)}, u32[]{:S(2)}) collective-permute-start(bf16[4,512,256]{2,1,0:T(8,128)(2,1)S(1)} %get-tuple-element.22), channel_id=1, source_target_pairs={{0,1},{1,0},{8,9},{9,8},{64,65},{65,64},{72,73},{73,72},{16,17},{1... | collective-permute-start | bytes 3145736 | tf_op jit(solution)/shard_map/ppermute | solution.py:39
  82.3 5.5 %collective-permute-start.35 = (f32[32,1024]{1,0:T(8,128)S(1)}, f32[32,1024]{1,0:T(8,128)S(1)}, u32[]{:S(2)}, u32[]{:S(2)}) collective-permute-start(f32[32,1024]{1,0:T(8,128)S(1)} %get-tuple-element.24), channel_id=1, source_target_pairs={{0,8},{1,9},{8,0},{9,1},{64,72},{65,73},{72,64},{73,65},{16,24},{1... | collective-permute-start | bytes 393224 | tf_op jit(solution)/shard_map/ppermute | solution.py:39
  83.4 14.5 %collective-permute-start.24 = (bf16[4,512,256]{2,1,0:T(8,128)(2,1)S(1)}, bf16[4,512,256]{2,1,0:T(8,128)(2,1)S(1)}, u32[]{:S(2)}, u32[]{:S(2)}) collective-permute-start(bf16[4,512,256]{2,1,0:T(8,128)(2,1)S(1)} %get-tuple-element.23), channel_id=1, source_target_pairs={{0,1},{1,0},{8,9},{9,8},{64,65},{65,64},{72,73},{73,72},{16,17},{1... | collective-permute-start | bytes 3145736 | tf_op jit(solution)/shard_map/ppermute | solution.py:39
  87.8 25.6 %collective-permute-start.36 = (f32[32,1024]{1,0:T(8,128)S(1)}, f32[32,1024]{1,0:T(8,128)S(1)}, u32[]{:S(2)}, u32[]{:S(2)}) collective-permute-start(f32[32,1024]{1,0:T(8,128)S(1)} %add.134), channel_id=1, source_target_pairs={{0,1},{1,0},{8,9},{9,8},{64,65},{65,64},{72,73},{73,72},{16,17},{1... | collective-permute-start | bytes 393224 | tf_op jit(solution)/shard_map/ppermute | solution.py:39
  87.9 11.9 %collective-permute-start.12 = (bf16[4,512,256]{2,1,0:T(8,128)(2,1)S(1)}, bf16[4,512,256]{2,1,0:T(8,128)(2,1)S(1)}, u32[]{:S(2)}, u32[]{:S(2)}) collective-permute-start(bf16[4,512,256]{2,1,0:T(8,128)(2,1)S(1)} %get-tuple-element.19), channel_id=1, source_target_pairs={{0,1},{1,0},{8,9},{9,8},{64,65},{65,64},{72,73},{73,72},{16,17},{1... | collective-permute-start | bytes 3145736 | tf_op jit(solution)/shard_map/ppermute | solution.py:39
  94.6 18.8 %collective-permute-start.13 = (bf16[512,256]{1,0:T(8,128)(2,1)S(1)}, bf16[512,256]{1,0:T(8,128)(2,1)S(1)}, u32[]{:S(2)}, u32[]{:S(2)}) collective-permute-start(bf16[512,256]{1,0:T(8,128)(2,1)S(1)} %get-tuple-element.34), channel_id=1, source_target_pairs={{0,2},{1,3},{8,10},{9,11},{64,66},{65,67},{72,74},{73,75},{16,18},... | collective-permute-start | bytes 786440 | tf_op jit(solution)/shard_map/ppermute | solution.py:39
  96.3 13.5 %collective-permute-start.25 = (bf16[512,256]{1,0:T(8,128)(2,1)S(1)}, bf16[512,256]{1,0:T(8,128)(2,1)S(1)}, u32[]{:S(2)}, u32[]{:S(2)}) collective-permute-start(bf16[512,256]{1,0:T(8,128)(2,1)S(1)} %get-tuple-element.30), channel_id=1, source_target_pairs={{0,2},{1,3},{8,10},{9,11},{64,66},{65,67},{72,74},{73,75},{16,18},... | collective-permute-start | bytes 786440 | tf_op jit(solution)/shard_map/ppermute | solution.py:39
  98.0 12.2 %collective-permute-start.29 = (bf16[512,256]{1,0:T(8,128)(2,1)S(1)}, bf16[512,256]{1,0:T(8,128)(2,1)S(1)}, u32[]{:S(2)}, u32[]{:S(2)}) collective-permute-start(bf16[512,256]{1,0:T(8,128)(2,1)S(1)} %get-tuple-element.27), channel_id=1, source_target_pairs={{0,6},{1,7},{8,14},{9,15},{64,70},{65,71},{72,78},{73,79},{16,22},... | collective-permute-start | bytes 786440 | tf_op jit(solution)/shard_map/ppermute | solution.py:39
  99.9 16.8 %collective-permute-start.17 = (bf16[512,256]{1,0:T(8,128)(2,1)S(1)}, bf16[512,256]{1,0:T(8,128)(2,1)S(1)}, u32[]{:S(2)}, u32[]{:S(2)}) collective-permute-start(bf16[512,256]{1,0:T(8,128)(2,1)S(1)} %get-tuple-element.31), channel_id=1, source_target_pairs={{0,6},{1,7},{8,14},{9,15},{64,70},{65,71},{72,78},{73,79},{16,22},... | collective-permute-start | bytes 786440 | tf_op jit(solution)/shard_map/ppermute | solution.py:39
  109.9 10.4 %collective-permute-start.27 = (bf16[512,256]{1,0:T(8,128)(2,1)S(1)}, bf16[512,256]{1,0:T(8,128)(2,1)S(1)}, u32[]{:S(2)}, u32[]{:S(2)}) collective-permute-start(bf16[512,256]{1,0:T(8,128)(2,1)S(1)} %get-tuple-element.28), channel_id=1, source_target_pairs={{0,2},{1,3},{8,10},{9,11},{64,66},{65,67},{72,74},{73,75},{16,18},... | collective-permute-start | bytes 786440 | tf_op jit(solution)/shard_map/ppermute | solution.py:39
  110.2 10.4 %collective-permute-start.28 = (bf16[512,256]{1,0:T(8,128)(2,1)S(1)}, bf16[512,256]{1,0:T(8,128)(2,1)S(1)}, u32[]{:S(2)}, u32[]{:S(2)}) collective-permute-start(bf16[512,256]{1,0:T(8,128)(2,1)S(1)} %get-tuple-element.29), channel_id=1, source_target_pairs={{0,6},{1,7},{8,14},{9,15},{64,70},{65,71},{72,78},{73,79},{16,22},... | collective-permute-start | bytes 786440 | tf_op jit(solution)/shard_map/ppermute | solution.py:39
  113.3 12.5 %collective-permute-start.26 = (bf16[512,256]{1,0:T(8,128)(2,1)S(1)}, bf16[512,256]{1,0:T(8,128)(2,1)S(1)}, u32[]{:S(2)}, u32[]{:S(2)}) collective-permute-start(bf16[512,256]{1,0:T(8,128)(2,1)S(1)} %fusion.1), channel_id=1, source_target_pairs={{0,2},{1,3},{8,10},{9,11},{64,66},{65,67},{72,74},{73,75},{16,18},... | collective-permute-start | bytes 786440 | tf_op jit(solution)/shard_map/ppermute | solution.py:39
  113.4 12.8 %collective-permute-start.30 = (bf16[512,256]{1,0:T(8,128)(2,1)S(1)}, bf16[512,256]{1,0:T(8,128)(2,1)S(1)}, u32[]{:S(2)}, u32[]{:S(2)}) collective-permute-start(bf16[512,256]{1,0:T(8,128)(2,1)S(1)} %fusion), channel_id=1, source_target_pairs={{0,6},{1,7},{8,14},{9,15},{64,70},{65,71},{72,78},{73,79},{16,22},... | collective-permute-start | bytes 786440 | tf_op jit(solution)/shard_map/ppermute | solution.py:39
  116.8 20.4 %collective-permute-start.15 = (bf16[512,256]{1,0:T(8,128)(2,1)S(1)}, bf16[512,256]{1,0:T(8,128)(2,1)S(1)}, u32[]{:S(2)}, u32[]{:S(2)}) collective-permute-start(bf16[512,256]{1,0:T(8,128)(2,1)S(1)} %get-tuple-element.32), channel_id=1, source_target_pairs={{0,2},{1,3},{8,10},{9,11},{64,66},{65,67},{72,74},{73,75},{16,18},... | collective-permute-start | bytes 786440 | tf_op jit(solution)/shard_map/ppermute | solution.py:39
  120.2 18.4 %collective-permute-start.16 = (bf16[512,256]{1,0:T(8,128)(2,1)S(1)}, bf16[512,256]{1,0:T(8,128)(2,1)S(1)}, u32[]{:S(2)}, u32[]{:S(2)}) collective-permute-start(bf16[512,256]{1,0:T(8,128)(2,1)S(1)} %get-tuple-element.33), channel_id=1, source_target_pairs={{0,6},{1,7},{8,14},{9,15},{64,70},{65,71},{72,78},{73,79},{16,22},... | collective-permute-start | bytes 786440 | tf_op jit(solution)/shard_map/ppermute | solution.py:39
  120.6 18.1 %collective-permute-start.14 = (bf16[512,256]{1,0:T(8,128)(2,1)S(1)}, bf16[512,256]{1,0:T(8,128)(2,1)S(1)}, u32[]{:S(2)}, u32[]{:S(2)}) collective-permute-start(bf16[512,256]{1,0:T(8,128)(2,1)S(1)} %fusion.3), channel_id=1, source_target_pairs={{0,2},{1,3},{8,10},{9,11},{64,66},{65,67},{72,74},{73,75},{16,18},... | collective-permute-start | bytes 786440 | tf_op jit(solution)/shard_map/ppermute | solution.py:39
  125.9 12.8 %collective-permute-start.18 = (bf16[512,256]{1,0:T(8,128)(2,1)S(1)}, bf16[512,256]{1,0:T(8,128)(2,1)S(1)}, u32[]{:S(2)}, u32[]{:S(2)}) collective-permute-start(bf16[512,256]{1,0:T(8,128)(2,1)S(1)} %fusion.2), channel_id=1, source_target_pairs={{0,6},{1,7},{8,14},{9,15},{64,70},{65,71},{72,78},{73,79},{16,22},... | collective-permute-start | bytes 786440 | tf_op jit(solution)/shard_map/ppermute | solution.py:39
  126.2 10.9 %collective-permute-start.37 = (f32[32,1024]{1,0:T(8,128)S(1)}, f32[32,1024]{1,0:T(8,128)S(1)}, u32[]{:S(2)}, u32[]{:S(2)}) collective-permute-start(f32[32,1024]{1,0:T(8,128)S(1)} %add.135), channel_id=1, source_target_pairs={{0,2},{1,3},{8,10},{9,11},{64,66},{65,67},{72,74},{73,75},{16,18},... | collective-permute-start | bytes 393224 | tf_op jit(solution)/shard_map/ppermute | solution.py:39
  137.1 14.9 %collective-permute-start.31 = (bf16[640,256]{1,0:T(8,128)(2,1)S(1)}, bf16[640,256]{1,0:T(8,128)(2,1)S(1)}, u32[]{:S(2)}, u32[]{:S(2)}) collective-permute-start(bf16[640,256]{1,0:T(8,128)(2,1)S(1)} %slice.157), channel_id=1, source_target_pairs={{0,72},{1,73},{8,64},{9,65},{64,8},{65,9},{72,0},{73,1},{16,88},{1... | collective-permute-start | bytes 983048 | tf_op jit(solution)/shard_map/ppermute | solution.py:39
  137.2 6.3 %copy-start.1 = (bf16[1024,512]{1,0:T(8,128)(2,1)S(1)}, bf16[1024,512]{1,0:T(8,128)(2,1)}, u32[]{:S(2)}) copy-start(bf16[1024,512]{1,0:T(8,128)(2,1)} %x_ref.3) | copy-start | bytes 3145732
  137.2 6.3 %collective-permute-start.38 = (f32[32,1024]{1,0:T(8,128)S(1)}, f32[32,1024]{1,0:T(8,128)S(1)}, u32[]{:S(2)}, u32[]{:S(2)}) collective-permute-start(f32[32,1024]{1,0:T(8,128)S(1)} %add.136.low_ref), channel_id=1, source_target_pairs={{0,6},{1,7},{8,14},{9,15},{64,70},{65,71},{72,78},{73,79},{16,22},... | collective-permute-start | bytes 393224 | tf_op jit(solution)/shard_map/ppermute | solution.py:39
  138.9 36.0 %copy-start.4 = (bf16[512,16]{0,1:T(8,128)(2,1)S(1)}, bf16[512,16]{0,1:T(8,128)(2,1)}, u32[]{:S(2)}) copy-start(bf16[512,16]{0,1:T(8,128)(2,1)} %param.9) | copy-start | bytes 49156
  138.9 28.9 %collective-permute-start.19 = (bf16[1024,256]{1,0:T(8,128)(2,1)S(1)}, bf16[1024,256]{1,0:T(8,128)(2,1)S(1)}, u32[]{:S(2)}, u32[]{:S(2)}) collective-permute-start(bf16[1024,256]{1,0:T(8,128)(2,1)S(1)} %shard_map.88.own_ref), channel_id=1, source_target_pairs={{8,0},{9,1},{64,72},{65,73},{24,16},{25,17},{80,88},{81,89},{40,32... | collective-permute-start | bytes 1572872 | tf_op jit(solution)/shard_map/ppermute | solution.py:39
  143.9 4.4 %collective-permute-start.39 = (f32[16,1152]{1,0:T(8,128)S(1)}, f32[16,1152]{1,0:T(8,128)S(1)}, u32[]{:S(2)}, u32[]{:S(2)}) collective-permute-start(f32[16,1152]{1,0:T(8,128)S(1)} %get-tuple-element.26), channel_id=1, source_target_pairs={{0,16},{1,17},{8,24},{9,25},{64,80},{65,81},{72,88},{73,89},{16,0}... | collective-permute-start | bytes 221192 | tf_op jit(solution)/shard_map/ppermute | solution.py:39
  148.3 6.1 %collective-permute-start.40 = (f32[16,1152]{1,0:T(8,128)S(1)}, f32[16,1152]{1,0:T(8,128)S(1)}, u32[]{:S(2)}, u32[]{:S(2)}) collective-permute-start(f32[16,1152]{1,0:T(8,128)S(1)} %add.137), channel_id=1, source_target_pairs={{0,48},{1,49},{8,56},{9,57},{64,112},{65,113},{72,120},{73,121},{1... | collective-permute-start | bytes 221192 | tf_op jit(solution)/shard_map/ppermute | solution.py:39
  152.1 22.8 %collective-permute-start.32 = (bf16[640,256]{1,0:T(8,128)(2,1)S(1)}, bf16[640,256]{1,0:T(8,128)(2,1)S(1)}, u32[]{:S(2)}, u32[]{:S(2)}) collective-permute-start(bf16[640,256]{1,0:T(8,128)(2,1)S(1)} %collective-permute-done.31.near_a), channel_id=1, source_target_pairs={{0,8},{1,9},{72,64},{73,65},{16,24},{17,25},{88,80},{89,81},{32,40... | collective-permute-start | bytes 983048 | tf_op jit(solution)/shard_map/ppermute | solution.py:39
  154.4 8.9 %collective-permute-start.41 = (f32[16,1152]{1,0:T(8,128)S(1)}, f32[16,1152]{1,0:T(8,128)S(1)}, u32[]{:S(2)}, u32[]{:S(2)}) collective-permute-start(f32[16,1152]{1,0:T(8,128)S(1)} %add.138), channel_id=1, source_target_pairs={{0,64},{1,65},{8,72},{9,73},{64,0},{65,1},{72,8},{73,9},{16,80},{1... | collective-permute-start | bytes 221192 | tf_op jit(solution)/shard_map/ppermute | solution.py:39
  163.9 9.2 %collective-permute-start.33 = (bf16[384,256]{1,0:T(8,128)(2,1)S(1)}, bf16[384,256]{1,0:T(8,128)(2,1)S(1)}, u32[]{:S(2)}, u32[]{:S(2)}) collective-permute-start(bf16[384,256]{1,0:T(8,128)(2,1)S(1)} %slice.158), channel_id=1, source_target_pairs={{0,64},{1,65},{72,8},{73,9},{16,80},{17,81},{88,24},{89,25},{32,96... | collective-permute-start | bytes 589832 | tf_op jit(solution)/shard_map/ppermute | solution.py:39
  165.2 9.7 %collective-permute-start.34 = (bf16[384,256]{1,0:T(8,128)(2,1)S(1)}, bf16[384,256]{1,0:T(8,128)(2,1)S(1)}, u32[]{:S(2)}, u32[]{:S(2)}) collective-permute-start(bf16[384,256]{1,0:T(8,128)(2,1)S(1)} %slice.158), channel_id=1, source_target_pairs={{8,64},{9,65},{64,8},{65,9},{24,80},{25,81},{80,24},{81,25},{40,96... | collective-permute-start | bytes 589832 | tf_op jit(solution)/shard_map/ppermute | solution.py:39
